TPU v7x, 32 devices: a whole 2x2x4 slice. The times are simulated.
32 devices in a mesh: seq: 8 (over z, x), head: 4 (over y, core).
Axes of the slice: x: 2, y: 2, z: 4, core: 2. Of those that a mesh axis runs over, the one named last changes fastest.
Arguments:
- queries: bfloat16 [4096, 6144], P('seq', 'head'), may hold values from -10 to 10
- keys: bfloat16 [4096, 6144], P('seq', 'head'), may hold values from -10 to 10
- values: bfloat16 [4096, 6144], P('seq', 'head'), may hold values from -6 to 6
- frame_of_block: int32 [16], P('seq'), may hold values from 0 to 7, never falling along the last dimension, each value on 1 to 4 neighbouring positions
- pair_mask: int32 [16, 16], P('seq'), may hold values 0 or 1
- w_out: bfloat16 [6144, 6144], P('head', 'seq'), may hold values from -0.4375 to 0.4375
Outputs:
- projected: bfloat16 [4096, 6144], P('seq', 'head')
Inputs may be any that keep to these rules, and one draw needn't show every extreme that they name: `frame_of_block`: frame ids never fall along the blocks, every frame spans 1 to 4 consecutive blocks.
All inputs are finite; a program needn't handle non-finite values. No bound on the sum of `pair_mask` on one device may be relied on, other than what follows from the above.
Results may differ from a plain program's by a relative error of at most 0.015.
Values may be sent and summed in bfloat16 or wider, within the bound.
No kernel may reach another device: no remote copies, remote signals or barrier semaphores. Data moves between devices by JAX's collectives and lax.ppermute only.
A program may use at most 192 MiB of HBM per device.

v0:
```python
import functools
import math

import jax
import jax.numpy as jnp
from jax import lax
from jax.experimental import pallas as pl
from jax.experimental.pallas import tpu as pltpu
from jax.sharding import PartitionSpec as P


HD = 128
BLK = 256
SPAN = 4
META = 16
BOTH = ("seq", "head")


def attention_kernel(devices, asked, tok, count, order, *refs):
    pieces, out, q_all, k_all, v_all, peak, total, accum, sems = (refs[:devices], *refs[devices:])

    @pl.when(count[0] > 0)
    def _():
        copies = []
        for d in range(devices):
            parts = ((k_all, 0), (v_all, tok), (q_all, 2 * tok + META))
            for part, (held, first) in enumerate(parts[: 3 if d < asked else 2]):
                copies.append(
                    pltpu.make_async_copy(
                        pieces[d].at[pl.ds(first, tok)], held.at[pl.ds(d * tok, tok)], sems.at[3 * d + part]
                    )
                )
        for copy in copies:
            copy.start()
        for copy in copies:
            copy.wait()
        factor = math.log2(math.e) / math.sqrt(HD)
        key_blocks = devices * tok // BLK

        @pl.loop(0, asked * tok // BLK)
        def _(index):
            rows = pl.ds(pl.multiple_of(index * BLK, BLK), BLK)
            q = q_all[rows, :]
            seen = count[index]
            peak[...] = jnp.full_like(peak, -jnp.inf)
            total[...] = jnp.zeros_like(total)
            accum[...] = jnp.zeros_like(accum)

            def update(step, number):
                firsts = [
                    pl.multiple_of(order[index * key_blocks + step + u] * BLK, BLK) for u in range(number)
                ]
                scores = [
                    lax.dot_general(
                        q, k_all[pl.ds(first, BLK), :], (((1,), (1,)), ((), ())), preferred_element_type=jnp.float32
                    )
                    for first in firsts
                ]
                top = functools.reduce(jnp.maximum, [s[:, i : i + HD] for s in scores for i in (0, HD)])
                old = peak[...]
                new = jnp.maximum(old, jnp.broadcast_to(jnp.max(top, axis=1, keepdims=True), old.shape))
                peak[...] = new
                fade = jnp.exp2((old - new) * factor)
                sums, mixed = None, None
                for first, score in zip(firsts, scores):
                    left = jnp.exp2((score[:, :HD] - new) * factor)
                    right = jnp.exp2((score[:, HD:] - new) * factor)
                    weight = jnp.concatenate([left.astype(jnp.bfloat16), right.astype(jnp.bfloat16)], axis=1)
                    term = jnp.dot(weight, v_all[pl.ds(first, BLK), :], preferred_element_type=jnp.float32)
                    sums = left + right if sums is None else sums + (left + right)
                    mixed = term if mixed is None else mixed + term
                total[...] = total[...] * fade + sums
                accum[...] = accum[...] * fade + mixed

            @pl.loop(0, seen // 4)
            def _(step):
                update(step * 4, 4)

            @pl.when((seen & 2) != 0)
            def _():
                update((seen // 4) * 4, 2)

            @pl.when((seen & 1) != 0)
            def _():
                update(seen - 1, 1)

            @pl.when(seen > 0)
            def _():
                out[rows, :] = (accum[...] / jnp.sum(total[...], axis=1, keepdims=True)).astype(out.dtype)


def attend_head(count, order, pieces, asked, tok):
    devices = len(pieces)
    rows, keys = asked * tok, devices * tok
    return pl.pallas_call(
        functools.partial(attention_kernel, devices, asked, tok),
        out_shape=jax.ShapeDtypeStruct((rows, HD), jnp.bfloat16),
        in_specs=[pl.BlockSpec(memory_space=pltpu.SMEM)] * 2 + [pl.BlockSpec(memory_space=pl.ANY)] * devices,
        out_specs=pl.BlockSpec(memory_space=pltpu.VMEM),
        scratch_shapes=[
            pltpu.VMEM((rows, HD), jnp.bfloat16),
            pltpu.VMEM((keys, HD), jnp.bfloat16),
            pltpu.VMEM((keys, HD), jnp.bfloat16),
            pltpu.VMEM((BLK, HD), jnp.float32),
            pltpu.VMEM((BLK, HD), jnp.float32),
            pltpu.VMEM((BLK, HD), jnp.float32),
            pltpu.SemaphoreType.DMA((3 * devices,)),
        ],
        compiler_params=pltpu.CompilerParams(vmem_limit_bytes=24 << 20),
        cost_estimate=pl.CostEstimate(
            flops=4 * rows * keys * HD, bytes_accessed=2 * HD * (2 * rows + 2 * keys), transcendentals=rows * keys
        ),
        name="attend_head",
    )(count, order, *pieces)


def pack_kernel(group, share, tok, own, keys, values, queries, meta, *refs):
    number = group * share
    whole, short = refs[:number], refs[number : 2 * number - group]
    held, in_sems, out_sems = refs[2 * number - group :]
    rows = ((keys, 0, tok), (values, tok, tok), (meta, 2 * tok, META), (queries, 2 * tok + META, tok))
    takes, puts = [], []
    for c in range(group):
        for t in range(share):
            i = c * share + t
            first = pl.multiple_of(((own[0] ^ c) * share + t) * HD, HD)
            takes.append(
                [
                    pltpu.make_async_copy(
                        source if source is meta else source.at[:, pl.ds(first, HD)],
                        held.at[i, pl.ds(start, size)],
                        in_sems.at[4 * i + part],
                    )
                    for part, (source, start, size) in enumerate(rows)
                ]
            )
            puts.append([pltpu.make_async_copy(held.at[i], whole[i], out_sems.at[2 * i])])
            if t:
                part = held.at[i, pl.ds(0, 2 * tok + META)]
                puts[i].append(pltpu.make_async_copy(part, short[i - c - 1], out_sems.at[2 * i + 1]))
    for i in [c * share + t for t in range(share) for c in range(group)]:
        for copy in takes[i]:
            copy.start()
    for i in [c * share + t for t in range(share) for c in range(group)]:
        for copy in takes[i]:
            copy.wait()
        for copy in puts[i]:
            copy.start()
    for pair in puts:
        for copy in pair:
            copy.wait()


def pack(own, keys, values, queries, meta, group, share):
    tok = keys.shape[0]
    number = group * share
    sizes = [3 * tok + META] * number + [2 * tok + META] * (number - group)
    packed = pl.pallas_call(
        functools.partial(pack_kernel, group, share, tok),
        out_shape=[jax.ShapeDtypeStruct((size, HD), jnp.bfloat16) for size in sizes],
        in_specs=[pl.BlockSpec(memory_space=pltpu.SMEM)] + [pl.BlockSpec(memory_space=pltpu.HBM)] * 4,
        out_specs=[pl.BlockSpec(memory_space=pltpu.HBM)] * (2 * number - group),
        scratch_shapes=[
            pltpu.VMEM((number, 3 * tok + META, HD), jnp.bfloat16),
            pltpu.SemaphoreType.DMA((4 * number,)),
            pltpu.SemaphoreType.DMA((2 * number,)),
        ],
        compiler_params=pltpu.CompilerParams(vmem_limit_bytes=60 << 20),
        name="pack",
    )(own[None], keys, values, queries, meta)
    split = lambda flat, each: [flat[c * each : (c + 1) * each] for c in range(group)]
    return split(packed[:number], share), [[None, *row] for row in split(packed[number:], share - 1)]


def block_lists(k_frame, rows, held):
    number = held.shape[0]
    q_frame = k_frame[: rows.shape[0]]
    pick = (held[:, None] == jnp.arange(rows.shape[1], dtype=jnp.int32)[None, :]).astype(jnp.int32)
    link = jnp.sum(rows[:, None, :] * pick[None, :, :], axis=2)
    same = k_frame[None, :] == q_frame[:, None]
    seen = ((k_frame[None, :] <= q_frame[:, None]) & ((link == 1) | same)).astype(jnp.int32)
    spot = jnp.arange(number, dtype=jnp.int32)
    before = (spot[:, None] < spot[None, :]).astype(jnp.int32)
    rank = jnp.sum(seen[:, :, None] * before[None, :, :], axis=1)
    chosen = seen[:, :, None] * (rank[:, :, None] == spot[None, None, :]).astype(jnp.int32)
    order = jnp.sum(chosen * spot[None, :, None], axis=1)
    return jnp.sum(seen, axis=1), order.reshape(-1)


def halves_body(queries, keys, values, frame_of_block, pair_mask, w_out, devices):
    group = devices // 2
    tok, width = queries.shape
    heads = width // HD
    share = heads // group
    per_dev = frame_of_block.shape[0]
    near = -(-(SPAN - 1) // per_dev)
    seq, head = lax.axis_index("seq"), lax.axis_index("head")
    own = lax.rem(seq, group)
    half, side, core = seq // group, head // 2, lax.rem(head, 2)

    meta = jnp.concatenate([frame_of_block[:, None], pair_mask], axis=1).astype(jnp.bfloat16)
    blocks = pair_mask.shape[1]
    meta = jnp.pad(meta, ((0, META - per_dev), (0, HD - 1 - blocks)))
    whole, short = pack(own, keys, values, queries, meta, group, share)

    arrived = [[row[0]] + [None] * (devices - 1) for row in [[whole[0][t]] for t in range(share)]]
    for t in range(share):
        for d in range(1, devices):
            if d < group:
                piece, senders = whole[d][t], range(group if t == 0 else devices)
            elif t == 0:
                piece, senders = whole[d % group][t], range(group, devices)
            else:
                piece, senders = short[d % group][t], range(group + near)
            arrived[t][d] = lax.ppermute(piece, "seq", [(s, s ^ d) for s in senders])

    meta_rows = slice(2 * tok, 2 * tok + per_dev)
    told = [piece[meta_rows, : 1 + blocks] for piece in arrived[1]]
    for d in range(group, devices):
        told[d] = jnp.where(half == 0, arrived[0][d][meta_rows, : 1 + blocks], told[d])
    told = jnp.concatenate(told, axis=0).astype(jnp.int32)
    source = seq ^ jnp.arange(devices, dtype=jnp.int32)
    held = (source[:, None] * per_dev + jnp.arange(per_dev, dtype=jnp.int32)).reshape(-1)
    count, order = block_lists(told[:, 0], told[:, 1:], held)
    count_all = jnp.where(half == 0, count, 0)

    columns = w_out.shape[1]
    w_here = jnp.concatenate(
        [lax.dynamic_slice_in_dim(w_out, (own ^ e) * share * HD, share * HD, 0) for e in range(group)], axis=0
    )
    bounds = [columns * p // 6 for p in (0, 1, 3, 5, 6)]
    w_parts = [w_here[:, first:last] for first, last in zip(bounds, bounds[1:])]
    w_far = [lax.ppermute(part, "seq", [(s, s ^ group) for s in range(devices)]) for part in w_parts]

    mixed = [None] * share
    both = attend_head(count_all, order, arrived[0], devices, tok)
    for t in range(1, share):
        mixed[t] = attend_head(count, order, arrived[t], group, tok)
    back = lax.ppermute(both[group * tok :], "seq", [(s, s ^ group) for s in range(group)])
    mixed[0] = jnp.where(half == 0, both[: group * tok], back)

    gathered = [mixed, [], [], []]
    for t in range(share):
        for e in (1, 2):
            gathered[e].append(lax.ppermute(mixed[t], "seq", [(s, s ^ e) for s in range(devices)]))
        gathered[3].append(lax.ppermute(gathered[2][t], "seq", [(s, s ^ 1) for s in range(devices)]))
    attn = jnp.concatenate(
        [
            jnp.concatenate(
                [gathered[e][t][(d ^ e) * tok : ((d ^ e) + 1) * tok] for e in range(group) for t in range(share)],
                axis=1,
            )
            for d in range(group)
        ],
        axis=0,
    )

    pairs = [(s, h) for s in range(devices) for h in range(4)]

    def place(s, h):
        return s * 4 + h

    def finish(weights, near_side):
        sides = [(s, h) for s, h in pairs if (h // 2 == s // group) == near_side]
        terms = jnp.dot(attn, weights, preferred_element_type=jnp.float32)
        kept = lax.dynamic_slice_in_dim(terms, core * 2 * tok, 2 * tok, 0)
        given = lax.dynamic_slice_in_dim(terms, (1 - core) * 2 * tok, 2 * tok, 0).astype(jnp.bfloat16)
        got = lax.ppermute(given, "head", [(h, h ^ 1) for h in range(4)])
        kept = kept + got.astype(jnp.float32)
        moves = [(place(s, h ^ 2), place(s, h)) for s, h in sides]
        other = lax.ppermute(kept.astype(jnp.bfloat16), BOTH, moves)
        summed = (kept + other.astype(jnp.float32)).astype(jnp.bfloat16)
        ends = []
        for flip in range(2):
            moves = [
                (place(s, h), place(s ^ ((h % 2) * 2 + flip), (h // 2) * 2 + (s % group) // 2)) for s, h in sides
            ]
            ends.append(lax.ppermute(summed[flip * tok : (flip + 1) * tok], BOTH, moves))
        return ends

    near_ends = finish(w_here, True)
    far_sets = [jnp.concatenate(w_far[:2], axis=1), w_far[2], w_far[3]]
    far_parts = [finish(w, False) for w in far_sets]
    far_ends = [jnp.concatenate([part[flip] for part in far_parts], axis=1) for flip in range(2)]
    same, across = [jnp.where(half == side, n, f) for n, f in zip(near_ends, far_ends)]
    odd = lax.rem(seq, 2) == 1
    return jnp.concatenate([jnp.where(odd, across, same), jnp.where(odd, same, across)], axis=1)


def gather_body(queries, keys, values, frame_of_block, pair_mask, w_out, devices):
    tok, width = queries.shape
    heads = width // HD
    per_dev = frame_of_block.shape[0]
    seq = lax.axis_index("seq")
    meta = lax.all_gather(jnp.concatenate([frame_of_block[:, None], pair_mask], axis=1), "seq", axis=0, tiled=True)
    source = seq ^ jnp.arange(devices, dtype=jnp.int32)
    held = (source[:, None] * per_dev + jnp.arange(per_dev, dtype=jnp.int32)).reshape(-1)
    pick = (held[:, None] == jnp.arange(devices * per_dev, dtype=jnp.int32)[None, :]).astype(jnp.int32)
    k_frame = jnp.sum(pick * meta[None, :, 0], axis=1)
    count, order = block_lists(k_frame, pair_mask, held)
    split = [x.reshape(tok, heads, HD).transpose(1, 0, 2) for x in (keys, values, queries)]
    stacked = jnp.concatenate(split[:2] + [jnp.zeros((heads, META, HD), jnp.bfloat16), split[2]], axis=1)
    pairs = [[(s, s ^ d) for s in range(devices)] for d in range(devices)]
    mixed = []
    for t in range(heads):
        row = [stacked[t]] + [lax.ppermute(stacked[t, : 2 * tok], "seq", pairs[d]) for d in range(1, devices)]
        mixed.append(attend_head(count, order, row, 1, tok))
    attn = jnp.concatenate(mixed, axis=1)
    weights = lax.all_gather(w_out, "seq", axis=1, tiled=True)
    terms = jnp.dot(attn, weights, preferred_element_type=jnp.float32)
    return lax.psum_scatter(terms.astype(jnp.bfloat16), "head", scatter_dimension=1, tiled=True)


def solution(mesh):
    devices, groups = mesh.shape["seq"], mesh.shape["head"]
    if devices & (devices - 1):
        raise ValueError("seq size")
    placed = (
        P("seq", "head"),
        P("seq", "head"),
        P("seq", "head"),
        P("seq"),
        P("seq", None),
        P("head", "seq"),
    )

    def program(*arrays):
        heads = arrays[0].shape[1] // HD // groups
        halves = (devices, groups) == (8, 4) and heads % (devices // 2) == 0

        def body(*blocks):
            if not halves:
                return gather_body(*blocks, devices)
            return halves_body(*blocks, devices)

        step = jax.shard_map(body, mesh=mesh, in_specs=placed, out_specs=P("seq", "head"), check_vma=False)
        return step(*arrays)

    return program
```

profile of v0, /device:TPU:0, one launch (start us, length us, event | category | flops | bytes accessed | tf_op | source)
XLA Modules:
  0.0 411.8 jit_solution(13940381405811704816)
XLA Ops:
  2.1 5.8 %pack.1 = (bf16[1552,128]{1,0:T(8,128)(2,1)}, bf16[1552,128]{1,0:T(8,128)(2,1)}, bf16[1552,128]{1,0:T(8,128)(2,1)}, bf16[1552,128]{1,0:T(8,128)(2,1)}, bf16[1552...) custom-call(s32[1]{0:T(128)} %bitcast.own, ...), custom_call_target="tpu_custom_call" | custom-call | tf_op jit(solution)/shard_map/pack/pallas_call | solution.py:158
  9.2 7.9 %collective-permute-start.10 = (bf16[1040,128]{1,0:T(8,128)(2,1)}, bf16[1040,128]{1,0:T(8,128)(2,1)S(1)}, u32[]{:S(2)}, u32[]{:S(2)}) collective-permute-start(bf16[1040,128]{1,0:T(8,128)(2,1)} %get-tuple-element.36), channel_id=1, source_target_pairs={{0,28},{4,24},{8,20},{12,16},{16,12},{20,8},{1,29},{5,25},{9,21},{... | collective-permute-start | bytes 798728 | tf_op jit(solution)/shard_map/ppermute | solution.py:215
  18.4 6.4 %collective-permute-start.8 = (bf16[1040,128]{1,0:T(8,128)(2,1)}, bf16[1040,128]{1,0:T(8,128)(2,1)S(1)}, u32[]{:S(2)}, u32[]{:S(2)}) collective-permute-start(bf16[1040,128]{1,0:T(8,128)(2,1)} %get-tuple-element.34), channel_id=1, source_target_pairs={{0,24},{4,28},{8,16},{12,20},{16,8},{20,12},{1,25},{5,29},{9,17},{... | collective-permute-start | bytes 798728 | tf_op jit(solution)/shard_map/ppermute | solution.py:215
  32.4 15.5 %collective-permute-start.1 = (bf16[1552,128]{1,0:T(8,128)(2,1)}, bf16[1552,128]{1,0:T(8,128)(2,1)S(1)}, u32[]{:S(2)}, u32[]{:S(2)}) collective-permute-start(bf16[1552,128]{1,0:T(8,128)(2,1)} %get-tuple-element.27), channel_id=1, source_target_pairs={{0,8},{4,12},{8,0},{12,4},{16,24},{20,28},{24,16},{28,20},{1,9},{5... | collective-permute-start | bytes 1191944 | tf_op jit(solution)/shard_map/ppermute | solution.py:215
  49.4 14.8 %collective-permute-start.6 = (bf16[1040,128]{1,0:T(8,128)(2,1)}, bf16[1040,128]{1,0:T(8,128)(2,1)S(1)}, u32[]{:S(2)}, u32[]{:S(2)}) collective-permute-start(bf16[1040,128]{1,0:T(8,128)(2,1)} %get-tuple-element.32), channel_id=1, source_target_pairs={{0,20},{4,16},{8,28},{12,24},{16,4},{20,0},{1,21},{5,17},{9,29},{1... | collective-permute-start | bytes 798728 | tf_op jit(solution)/shard_map/ppermute | solution.py:215
  77.9 9.2 %collective-permute-done.2.refs_3_ = bf16[1552,128]{1,0:T(8,128)(2,1)S(1)} collective-permute-done((bf16[1552,128]{1,0:T(8,128)(2,1)}, bf16[1552,128]{1,0:T(8,128)(2,1)S(1)}, u32[]{:S(2)}, u32[]{:S(2)}) %collective-permute-start.2) | collective-permute-done | bytes 397344 | tf_op jit(solution)/shard_map/ppermute | solution.py:215
  102.0 6.0 %collective-permute-done.4.refs_4_ = bf16[1040,128]{1,0:T(8,128)(2,1)S(1)} collective-permute-done((bf16[1040,128]{1,0:T(8,128)(2,1)}, bf16[1040,128]{1,0:T(8,128)(2,1)S(1)}, u32[]{:S(2)}, u32[]{:S(2)}) %collective-permute-start.4) | collective-permute-done | bytes 266272 | tf_op jit(solution)/shard_map/ppermute | solution.py:215
  113.7 8.6 %collective-permute-done.12.refs_2_ = bf16[1552,128]{1,0:T(8,128)(2,1)} collective-permute-done((bf16[1552,128]{1,0:T(8,128)(2,1)}, bf16[1552,128]{1,0:T(8,128)(2,1)}, u32[]{:S(2)}, u32[]{:S(2)}) %collective-permute-start.12) | collective-permute-done | bytes 397344 | tf_op jit(solution)/shard_map/ppermute | solution.py:215
  124.3 12.8 %collective-permute-done.13.refs_3_ = bf16[1552,128]{1,0:T(8,128)(2,1)} collective-permute-done((bf16[1552,128]{1,0:T(8,128)(2,1)}, bf16[1552,128]{1,0:T(8,128)(2,1)}, u32[]{:S(2)}, u32[]{:S(2)}) %collective-permute-start.13) | collective-permute-done | bytes 397344 | tf_op jit(solution)/shard_map/ppermute | solution.py:215
  140.1 29.9 %attend_head.3 = bf16[4096,128]{1,0:T(8,128)(2,1)S(1)} custom-call(s32[16]{0:T(128)S(1)} %broadcast_select_fusion.6.count, s32[256]{0:T(256)S(1)} %reshape.123.order, bf16[1552,128]{1,0:T(8,128)(2,1)S(1)} %copy-done.7, bf16[1552,128]{1,0:T(8,128)(2,1)S(1)} %copy-done.13, bf16[1552,128]{1,0:T(8,128)(2,1)} %collective-permute-done.12.refs_2_, ...), custom_call_target="tpu_custom_call" | custom-call | flops 8589934592 | bytes 4194304 | tf_op jit(solution)/shard_map/attend_head/pallas_call | solution.py:95
  175.0 13.5 %attend_head.4 = bf16[2048,128]{1,0:T(8,128)(2,1)S(1)} custom-call(s32[16]{0:T(128)S(1)} %get-tuple-element.45.count, s32[256]{0:T(256)S(1)} %reshape.123.order, bf16[1552,128]{1,0:T(8,128)(2,1)S(1)} %copy-done.3, bf16[1552,128]{1,0:T(8,128)(2,1)S(1)} %copy-done.5, bf16[1552,128]{1,0:T(8,128)(2,1)S(1)} %copy-done.9, bf16[1552,128]{1,0:T(8,128)(2,1)S(1)} %copy-done.11, ...), custom_call_target="tpu_custom_call" | custom-call | flops 4294967296 | bytes 3145728 | tf_op jit(solution)/shard_map/attend_head/pallas_call | solution.py:95
  190.0 10.4 %collective-permute-start.21 = (bf16[1040,128]{1,0:T(8,128)(2,1)S(1)}, bf16[1040,128]{1,0:T(8,128)(2,1)S(1)}, u32[]{:S(2)}, u32[]{:S(2)}) collective-permute-start(bf16[1040,128]{1,0:T(8,128)(2,1)S(1)} %copy-done.31), channel_id=1, source_target_pairs={{0,28},{4,24},{8,20},{12,16},{16,12},{20,8},{1,29},{5,25},{9,21},{... | collective-permute-start | bytes 798728 | tf_op jit(solution)/shard_map/ppermute | solution.py:215
  208.9 8.2 %collective-permute-start.26 = (bf16[2048,128]{1,0:T(8,128)(2,1)S(1)}, bf16[2048,128]{1,0:T(8,128)(2,1)S(1)}, u32[]{:S(2)}, u32[]{:S(2)}) collective-permute-start(bf16[2048,128]{1,0:T(8,128)(2,1)S(1)} %attend_head.4), channel_id=1, source_target_pairs={{0,8},{4,12},{8,0},{12,4},{16,24},{20,28},{24,16},{28,20},{1,9},{5... | collective-permute-start | bytes 1572872 | tf_op jit(solution)/shard_map/ppermute | solution.py:245
  218.2 12.4 %attend_head.5 = bf16[2048,128]{1,0:T(8,128)(2,1)S(1)} custom-call(s32[16]{0:T(128)S(1)} %get-tuple-element.45.count, s32[256]{0:T(256)S(1)} %reshape.123.order, bf16[1552,128]{1,0:T(8,128)(2,1)S(1)} %copy-done.2, bf16[1552,128]{1,0:T(8,128)(2,1)} %collective-permute-done.15.refs_1_, bf16[1552,128]{1,0:T(8,128)(2,1)} %collective-permute-done.16.refs_2_, ...), custom_call_target="tpu_custom_call" | custom-call | flops 4294967296 | bytes 3145728 | tf_op jit(solution)/shard_map/attend_head/pallas_call | solution.py:95
  234.3 10.5 %collective-permute-start.35 = (bf16[1536,256]{1,0:T(8,128)(2,1)S(1)}, bf16[1536,256]{1,0:T(8,128)(2,1)S(1)}, u32[]{:S(2)}, u32[]{:S(2)}) collective-permute-start(bf16[1536,256]{1,0:T(8,128)(2,1)S(1)} %copy-done.27), channel_id=1, source_target_pairs={{0,16},{4,20},{8,24},{12,28},{16,0},{20,4},{24,8},{28,12},{1,17},{... | collective-permute-start | bytes 2359304 | tf_op jit(solution)/shard_map/ppermute | solution.py:233
  244.9 8.4 %collective-permute-start.34 = (bf16[1536,128]{1,0:T(8,128)(2,1)S(1)}, bf16[1536,128]{1,0:T(8,128)(2,1)S(1)}, u32[]{:S(2)}, u32[]{:S(2)}) collective-permute-start(bf16[1536,128]{1,0:T(8,128)(2,1)S(1)} %copy-done.29), channel_id=1, source_target_pairs={{0,16},{4,20},{8,24},{12,28},{16,0},{20,4},{24,8},{28,12},{1,17},{... | collective-permute-start | bytes 1179656 | tf_op jit(solution)/shard_map/ppermute | solution.py:233
  254.4 13.1 %collective-permute-done.27 = bf16[2048,128]{1,0:T(8,128)(2,1)S(1)} collective-permute-done((bf16[2048,128]{1,0:T(8,128)(2,1)S(1)}, bf16[2048,128]{1,0:T(8,128)(2,1)S(1)}, u32[]{:S(2)}, u32[]{:S(2)}) %collective-permute-start.27) | collective-permute-done | bytes 524320 | tf_op jit(solution)/shard_map/ppermute | solution.py:245
  268.5 7.7 %collective-permute-done.25 = bf16[2048,128]{1,0:T(8,128)(2,1)S(1)} collective-permute-done((bf16[2048,128]{1,0:T(8,128)(2,1)S(1)}, bf16[2048,128]{1,0:T(8,128)(2,1)S(1)}, u32[]{:S(2)}, u32[]{:S(2)}) %collective-permute-start.25) | collective-permute-done | bytes 524320 | tf_op jit(solution)/shard_map/ppermute | solution.py:245
  277.9 10.0 %collective-permute-done.28 = bf16[2048,128]{1,0:T(8,128)(2,1)S(1)} collective-permute-done((bf16[2048,128]{1,0:T(8,128)(2,1)S(1)}, bf16[2048,128]{1,0:T(8,128)(2,1)S(1)}, u32[]{:S(2)}, u32[]{:S(2)}) %collective-permute-start.28) | collective-permute-done | bytes 524320 | tf_op jit(solution)/shard_map/ppermute | solution.py:246
  296.5 25.7 %collective-permute-done.34 = bf16[1536,128]{1,0:T(8,128)(2,1)S(1)} collective-permute-done((bf16[1536,128]{1,0:T(8,128)(2,1)S(1)}, bf16[1536,128]{1,0:T(8,128)(2,1)S(1)}, u32[]{:S(2)}, u32[]{:S(2)}) %collective-permute-start.34) | collective-permute-done | bytes 393248 | tf_op jit(solution)/shard_map/ppermute | solution.py:233
  326.6 12.5 %collective-permute-done.39 = bf16[1536,256]{1,0:T(8,128)(2,1)} collective-permute-done((bf16[1536,256]{1,0:T(8,128)(2,1)S(1)}, bf16[1536,256]{1,0:T(8,128)(2,1)}, u32[]{:S(2)}, u32[]{:S(2)}) %collective-permute-start.39) | collective-permute-done | bytes 786464 | tf_op jit(solution)/shard_map/ppermute | solution.py:233
  363.2 6.0 %collective-permute-start.37 = (bf16[1024,384]{1,0:T(8,128)(2,1)S(1)}, bf16[1024,384]{1,0:T(8,128)(2,1)S(1)}, u32[]{:S(2)}, u32[]{:S(2)}) collective-permute-start(bf16[1024,384]{1,0:T(8,128)(2,1)S(1)} %fusion.5), channel_id=1, source_target_pairs={{0,2},{1,3},{4,6},{5,7},{8,10},{9,11},{12,14},{13,15},{18,16},{19,... | collective-permute-start | bytes 2359304 | tf_op jit(solution)/shard_map/ppermute | solution.py:271
  373.8 12.4 %collective-permute-done.32 = bf16[1024,768]{1,0:T(8,128)(2,1)S(1)} collective-permute-done((bf16[1024,768]{1,0:T(8,128)(2,1)S(1)}, bf16[1024,768]{1,0:T(8,128)(2,1)S(1)}, u32[]{:S(2)}, u32[]{:S(2)}) %collective-permute-start.32) | collective-permute-done | bytes 1572896 | tf_op jit(solution)/shard_map/ppermute | solution.py:271
  395.4 13.5 %collective-permute-done.33 = bf16[512,768]{1,0:T(8,128)(2,1)S(1)} collective-permute-done((bf16[512,768]{1,0:T(8,128)(2,1)S(1)}, bf16[512,768]{1,0:T(8,128)(2,1)S(1)}, u32[]{:S(2)}, u32[]{:S(2)}) %collective-permute-start.33) | collective-permute-done | bytes 786464 | tf_op jit(solution)/shard_map/ppermute | solution.py:278
  (215 shorter events, 129.8 us)
Async XLA Ops:
  7.9 41.5 %collective-permute-start.9 = (bf16[1552,128]{1,0:T(8,128)(2,1)}, bf16[1552,128]{1,0:T(8,128)(2,1)S(1)}, u32[]{:S(2)}, u32[]{:S(2)}) collective-permute-start(bf16[1552,128]{1,0:T(8,128)(2,1)} %get-tuple-element.35), channel_id=1, source_target_pairs={{16,12},{20,8},{24,4},{28,0},{17,13},{21,9},{25,5},{29,1},{18,14},... | collective-permute-start | bytes 1191944 | tf_op jit(solution)/shard_map/ppermute | solution.py:215
  17.1 47.0 %collective-permute-start.7 = (bf16[1552,128]{1,0:T(8,128)(2,1)}, bf16[1552,128]{1,0:T(8,128)(2,1)S(1)}, u32[]{:S(2)}, u32[]{:S(2)}) collective-permute-start(bf16[1552,128]{1,0:T(8,128)(2,1)} %get-tuple-element.33), channel_id=1, source_target_pairs={{16,8},{20,12},{24,0},{28,4},{17,9},{21,13},{25,1},{29,5},{18,10},... | collective-permute-start | bytes 1191944 | tf_op jit(solution)/shard_map/ppermute | solution.py:215
  24.8 44.8 %collective-permute-start = (bf16[1552,128]{1,0:T(8,128)(2,1)}, bf16[1552,128]{1,0:T(8,128)(2,1)S(1)}, u32[]{:S(2)}, u32[]{:S(2)}) collective-permute-start(bf16[1552,128]{1,0:T(8,128)(2,1)} %get-tuple-element.26), channel_id=1, source_target_pairs={{0,4},{4,0},{8,12},{12,8},{16,20},{20,16},{24,28},{28,24},{1,5},{5... | collective-permute-start | bytes 1191944 | tf_op jit(solution)/shard_map/ppermute | solution.py:215
  32.4 38.5 %collective-permute-start.1 = (bf16[1552,128]{1,0:T(8,128)(2,1)}, bf16[1552,128]{1,0:T(8,128)(2,1)S(1)}, u32[]{:S(2)}, u32[]{:S(2)}) collective-permute-start(bf16[1552,128]{1,0:T(8,128)(2,1)} %get-tuple-element.27), channel_id=1, source_target_pairs={{0,8},{4,12},{8,0},{12,4},{16,24},{20,28},{24,16},{28,20},{1,9},{5... | collective-permute-start | bytes 1191944 | tf_op jit(solution)/shard_map/ppermute | solution.py:215
  48.0 49.1 %collective-permute-start.5 = (bf16[1552,128]{1,0:T(8,128)(2,1)}, bf16[1552,128]{1,0:T(8,128)(2,1)S(1)}, u32[]{:S(2)}, u32[]{:S(2)}) collective-permute-start(bf16[1552,128]{1,0:T(8,128)(2,1)} %get-tuple-element.31), channel_id=1, source_target_pairs={{16,4},{20,0},{24,12},{28,8},{17,5},{21,1},{25,13},{29,9},{18,6},{... | collective-permute-start | bytes 1191944 | tf_op jit(solution)/shard_map/ppermute | solution.py:215
  49.4 45.9 %collective-permute-start.6 = (bf16[1040,128]{1,0:T(8,128)(2,1)}, bf16[1040,128]{1,0:T(8,128)(2,1)S(1)}, u32[]{:S(2)}, u32[]{:S(2)}) collective-permute-start(bf16[1040,128]{1,0:T(8,128)(2,1)} %get-tuple-element.32), channel_id=1, source_target_pairs={{0,20},{4,16},{8,28},{12,24},{16,4},{20,0},{1,21},{5,17},{9,29},{1... | collective-permute-start | bytes 798728 | tf_op jit(solution)/shard_map/ppermute | solution.py:215
  69.6 39.5 %collective-permute-start.3 = (bf16[1552,128]{1,0:T(8,128)(2,1)S(1)}, bf16[1552,128]{1,0:T(8,128)(2,1)S(1)}, u32[]{:S(2)}, u32[]{:S(2)}) collective-permute-start(bf16[1552,128]{1,0:T(8,128)(2,1)S(1)} %copy-done.6), channel_id=1, source_target_pairs={{16,0},{20,4},{24,8},{28,12},{17,1},{21,5},{25,9},{29,13},{18,2},{... | collective-permute-start | bytes 1191944 | tf_op jit(solution)/shard_map/ppermute | solution.py:215
  70.9 37.1 %collective-permute-start.4 = (bf16[1040,128]{1,0:T(8,128)(2,1)}, bf16[1040,128]{1,0:T(8,128)(2,1)S(1)}, u32[]{:S(2)}, u32[]{:S(2)}) collective-permute-start(bf16[1040,128]{1,0:T(8,128)(2,1)} %get-tuple-element.30), channel_id=1, source_target_pairs={{0,16},{4,20},{8,24},{12,28},{16,0},{20,4},{1,17},{5,21},{9,25},{1... | collective-permute-start | bytes 798728 | tf_op jit(solution)/shard_map/ppermute | solution.py:215
  97.2 39.9 %collective-permute-start.13 = (bf16[1552,128]{1,0:T(8,128)(2,1)}, bf16[1552,128]{1,0:T(8,128)(2,1)}, u32[]{:S(2)}, u32[]{:S(2)}) collective-permute-start(bf16[1552,128]{1,0:T(8,128)(2,1)} %get-tuple-element.35), channel_id=1, source_target_pairs={{0,12},{4,8},{8,4},{12,0},{1,13},{5,9},{9,5},{13,1},{2,14},{6,10},... | collective-permute-start | bytes 1191944 | tf_op jit(solution)/shard_map/ppermute | solution.py:215
  108.0 109.1 %collective-permute-start.15 = (bf16[1552,128]{1,0:T(8,128)(2,1)}, bf16[1552,128]{1,0:T(8,128)(2,1)}, u32[]{:S(2)}, u32[]{:S(2)}) collective-permute-start(bf16[1552,128]{1,0:T(8,128)(2,1)} %get-tuple-element.38), channel_id=1, source_target_pairs={{0,4},{4,0},{8,12},{12,8},{16,20},{20,16},{24,28},{28,24},{1,5},{5... | collective-permute-start | bytes 1191944 | tf_op jit(solution)/shard_map/ppermute | solution.py:215
  109.1 109.1 %collective-permute-start.16 = (bf16[1552,128]{1,0:T(8,128)(2,1)}, bf16[1552,128]{1,0:T(8,128)(2,1)}, u32[]{:S(2)}, u32[]{:S(2)}) collective-permute-start(bf16[1552,128]{1,0:T(8,128)(2,1)} %get-tuple-element.39), channel_id=1, source_target_pairs={{0,8},{4,12},{8,0},{12,4},{16,24},{20,28},{24,16},{28,20},{1,9},{5... | collective-permute-start | bytes 1191944 | tf_op jit(solution)/shard_map/ppermute | solution.py:215
  111.8 76.7 %collective-permute-start.18 = (bf16[1040,128]{1,0:T(8,128)(2,1)}, bf16[1040,128]{1,0:T(8,128)(2,1)}, u32[]{:S(2)}, u32[]{:S(2)}) collective-permute-start(bf16[1040,128]{1,0:T(8,128)(2,1)} %get-tuple-element.41), channel_id=1, source_target_pairs={{0,16},{4,20},{8,24},{12,28},{16,0},{20,4},{1,17},{5,21},{9,25},{1... | collective-permute-start | bytes 798728 | tf_op jit(solution)/shard_map/ppermute | solution.py:215
  122.4 66.3 %collective-permute-start.19 = (bf16[1040,128]{1,0:T(8,128)(2,1)}, bf16[1040,128]{1,0:T(8,128)(2,1)}, u32[]{:S(2)}, u32[]{:S(2)}) collective-permute-start(bf16[1040,128]{1,0:T(8,128)(2,1)} %get-tuple-element.42), channel_id=1, source_target_pairs={{0,20},{4,16},{8,28},{12,24},{16,4},{20,0},{1,21},{5,17},{9,29},{1... | collective-permute-start | bytes 798728 | tf_op jit(solution)/shard_map/ppermute | solution.py:215
  208.9 44.4 %collective-permute-start.26 = (bf16[2048,128]{1,0:T(8,128)(2,1)S(1)}, bf16[2048,128]{1,0:T(8,128)(2,1)S(1)}, u32[]{:S(2)}, u32[]{:S(2)}) collective-permute-start(bf16[2048,128]{1,0:T(8,128)(2,1)S(1)} %attend_head.4), channel_id=1, source_target_pairs={{0,8},{4,12},{8,0},{12,4},{16,24},{20,28},{24,16},{28,20},{1,9},{5... | collective-permute-start | bytes 1572872 | tf_op jit(solution)/shard_map/ppermute | solution.py:245
  231.6 35.8 %collective-permute-start.27 = (bf16[2048,128]{1,0:T(8,128)(2,1)S(1)}, bf16[2048,128]{1,0:T(8,128)(2,1)S(1)}, u32[]{:S(2)}, u32[]{:S(2)}) collective-permute-start(bf16[2048,128]{1,0:T(8,128)(2,1)S(1)} %attend_head.5), channel_id=1, source_target_pairs={{0,8},{4,12},{8,0},{12,4},{16,24},{20,28},{24,16},{28,20},{1,9},{5... | collective-permute-start | bytes 1572872 | tf_op jit(solution)/shard_map/ppermute | solution.py:245
  231.9 44.3 %collective-permute-start.25 = (bf16[2048,128]{1,0:T(8,128)(2,1)S(1)}, bf16[2048,128]{1,0:T(8,128)(2,1)S(1)}, u32[]{:S(2)}, u32[]{:S(2)}) collective-permute-start(bf16[2048,128]{1,0:T(8,128)(2,1)S(1)} %slice_select_fusion), channel_id=1, source_target_pairs={{0,8},{4,12},{8,0},{12,4},{16,24},{20,28},{24,16},{28,20},{1,9},{5... | collective-permute-start | bytes 1572872 | tf_op jit(solution)/shard_map/ppermute | solution.py:245
  234.3 87.9 %collective-permute-start.35 = (bf16[1536,256]{1,0:T(8,128)(2,1)S(1)}, bf16[1536,256]{1,0:T(8,128)(2,1)S(1)}, u32[]{:S(2)}, u32[]{:S(2)}) collective-permute-start(bf16[1536,256]{1,0:T(8,128)(2,1)S(1)} %copy-done.27), channel_id=1, source_target_pairs={{0,16},{4,20},{8,24},{12,28},{16,0},{20,4},{24,8},{28,12},{1,17},{... | collective-permute-start | bytes 2359304 | tf_op jit(solution)/shard_map/ppermute | solution.py:233
  244.9 77.2 %collective-permute-start.34 = (bf16[1536,128]{1,0:T(8,128)(2,1)S(1)}, bf16[1536,128]{1,0:T(8,128)(2,1)S(1)}, u32[]{:S(2)}, u32[]{:S(2)}) collective-permute-start(bf16[1536,128]{1,0:T(8,128)(2,1)S(1)} %copy-done.29), channel_id=1, source_target_pairs={{0,16},{4,20},{8,24},{12,28},{16,0},{20,4},{24,8},{28,12},{1,17},{... | collective-permute-start | bytes 1179656 | tf_op jit(solution)/shard_map/ppermute | solution.py:233
  253.3 34.8 %collective-permute-start.29 = (bf16[2048,128]{1,0:T(8,128)(2,1)S(1)}, bf16[2048,128]{1,0:T(8,128)(2,1)S(1)}, u32[]{:S(2)}, u32[]{:S(2)}) collective-permute-start(bf16[2048,128]{1,0:T(8,128)(2,1)S(1)} %collective-permute-done.26), channel_id=1, source_target_pairs={{0,4},{4,0},{8,12},{12,8},{16,20},{20,16},{24,28},{28,24},{1,5},{5... | collective-permute-start | bytes 1572872 | tf_op jit(solution)/shard_map/ppermute | solution.py:246
  287.9 51.2 %collective-permute-start.39 = (bf16[1536,256]{1,0:T(8,128)(2,1)S(1)}, bf16[1536,256]{1,0:T(8,128)(2,1)}, u32[]{:S(2)}, u32[]{:S(2)}) collective-permute-start(bf16[1536,256]{1,0:T(8,128)(2,1)S(1)} %copy-done.26), channel_id=1, source_target_pairs={{0,16},{4,20},{8,24},{12,28},{16,0},{20,4},{24,8},{28,12},{1,17},{... | collective-permute-start | bytes 2359304 | tf_op jit(solution)/shard_map/ppermute | solution.py:233
  288.1 56.9 %collective-permute-start.43 = (bf16[1536,128]{1,0:T(8,128)(2,1)S(1)}, bf16[1536,128]{1,0:T(8,128)(2,1)S(1)}, u32[]{:S(2)}, u32[]{:S(2)}) collective-permute-start(bf16[1536,128]{1,0:T(8,128)(2,1)S(1)} %copy-done.28), channel_id=1, source_target_pairs={{0,16},{4,20},{8,24},{12,28},{16,0},{20,4},{24,8},{28,12},{1,17},{... | collective-permute-start | bytes 1179656 | tf_op jit(solution)/shard_map/ppermute | solution.py:233
  325.8 37.2 %collective-permute-start.36 = (bf16[1024,384]{1,0:T(8,128)(2,1)S(1)}, bf16[1024,384]{1,0:T(8,128)(2,1)S(1)}, u32[]{:S(2)}, u32[]{:S(2)}) collective-permute-start(bf16[1024,384]{1,0:T(8,128)(2,1)S(1)} %dynamic-slice_convert_fusion.1), channel_id=1, source_target_pairs={{0,1},{1,0},{2,3},{3,2},{4,5},{5,4},{6,7},{7,6},{8,9},{9,8},{10,11... | collective-permute-start | bytes 2359304 | tf_op jit(solution)/shard_map/ppermute | solution.py:268
  347.5 38.7 %collective-permute-start.32 = (bf16[1024,768]{1,0:T(8,128)(2,1)S(1)}, bf16[1024,768]{1,0:T(8,128)(2,1)S(1)}, u32[]{:S(2)}, u32[]{:S(2)}) collective-permute-start(bf16[1024,768]{1,0:T(8,128)(2,1)S(1)} %fusion), channel_id=1, source_target_pairs={{2,0},{3,1},{6,4},{7,5},{10,8},{11,9},{14,12},{15,13},{16,18},{17,... | collective-permute-start | bytes 4718600 | tf_op jit(solution)/shard_map/ppermute | solution.py:271
  360.4 31.5 %collective-permute-start.46 = (bf16[512,128]{1,0:T(8,128)(2,1)S(1)}, bf16[512,128]{1,0:T(8,128)(2,1)}, u32[]{:S(2)}, u32[]{:S(2)}) collective-permute-start(bf16[512,128]{1,0:T(8,128)(2,1)S(1)} %get-tuple-element.111), channel_id=1, source_target_pairs={{2,6},{3,14},{6,2},{7,10},{10,15},{11,7},{14,11},{15,3},{16,20},{1... | collective-permute-start | bytes 393224 | tf_op jit(solution)/shard_map/ppermute | solution.py:278
  (60 other events, 808.2 us)
where the time goes:
time: 413 us; the launch traced here: 412 us
  starting transfers between devices  155 us (38%)
  waiting for transfers between devices  154 us (37%)
  Pallas kernels  61.5 us (15%)
  local copies, waits for them, and re-layouts  17.7 us (4%)
  matrix products  13.6 us (3%)
  other arithmetic  9.29 us (2%)
    ppermute x21, starting transfers between devices, halves_body(): arrived[t][d] = lax.ppermute(piece, 'seq', [(s, s ^ d) for s in senders])  89.5 us
    pallas_call x3, Pallas kernels, attend_head(): pl.pallas_call(functools.partial(attention_kernel, devices, asked, tok),...  55.8 us
    ppermute x21, waiting for transfers between devices, halves_body(): arrived[t][d] = lax.ppermute(piece, 'seq', [(s, s ^ d) for s in senders])  48.5 us
    ppermute x4, waiting for transfers between devices, halves_body(): lax.ppermute(part, 'seq', [(s, s ^ group) for s in range(devices)])  40.9 us
    ppermute x4, starting transfers between devices, halves_body(): lax.ppermute(part, 'seq', [(s, s ^ group) for s in range(devices)])  21.8 us
    ppermute x6, waiting for transfers between devices, halves_body(): lax.ppermute(mixed[t], 'seq', [(s, s ^ e) for s in range(devices)])  20.8 us
    ppermute x4, waiting for transfers between devices, finish(): other = lax.ppermute(kept.astype(jnp.bfloat16), BOTH, moves)  19.9 us
    dot_general x4, matrix products, finish(): terms = jnp.dot(attn, weights, preferred_element_type=jnp.float32)  13.6 us
  transfers between devices with their start and end apart: 51, of which 17 were waited for; matrix products, arithmetic and copies ran while one was open for 6% of the time, Pallas kernels for 14%

commit v1 on v0

--- a/solution.py
+++ b/solution.py
@@ -255,34 +255,34 @@
         axis=0,
     )
 
-    pairs = [(s, h) for s in range(devices) for h in range(4)]
-
     def place(s, h):
         return s * 4 + h
 
-    def finish(weights, near_side):
-        sides = [(s, h) for s, h in pairs if (h // 2 == s // group) == near_side]
+    def moves(flip, turn):
+        return [
+            (place(s, h), place(s ^ ((h % 2) * 2 + flip), ((h // 2) ^ turn) * 2 + (s % group) // 2))
+            for s in range(devices)
+            for h in range(4)
+        ]
+
+    ends = [[], []]
+    for p in range(2):
+        first, last = bounds[2 * p], bounds[2 * p + 2]
+        weights = jnp.concatenate([w_here[:, first:last], *w_far[2 * p : 2 * p + 2]], axis=1)
+        if p:
+            weights = lax.optimization_barrier((weights, parts))[0]
         terms = jnp.dot(attn, weights, preferred_element_type=jnp.float32)
         kept = lax.dynamic_slice_in_dim(terms, core * 2 * tok, 2 * tok, 0)
         given = lax.dynamic_slice_in_dim(terms, (1 - core) * 2 * tok, 2 * tok, 0).astype(jnp.bfloat16)
         got = lax.ppermute(given, "head", [(h, h ^ 1) for h in range(4)])
-        kept = kept + got.astype(jnp.float32)
-        moves = [(place(s, h ^ 2), place(s, h)) for s, h in sides]
-        other = lax.ppermute(kept.astype(jnp.bfloat16), BOTH, moves)
-        summed = (kept + other.astype(jnp.float32)).astype(jnp.bfloat16)
-        ends = []
+        summed = (kept + got.astype(jnp.float32)).astype(jnp.bfloat16)
+        here, far = summed[:, : last - first], summed[:, last - first :]
+        parts = (jnp.where(half == side, here, far), jnp.where(half == side, far, here))
         for flip in range(2):
-            moves = [
-                (place(s, h), place(s ^ ((h % 2) * 2 + flip), (h // 2) * 2 + (s % group) // 2)) for s, h in sides
-            ]
-            ends.append(lax.ppermute(summed[flip * tok : (flip + 1) * tok], BOTH, moves))
-        return ends
-
-    near_ends = finish(w_here, True)
-    far_sets = [jnp.concatenate(w_far[:2], axis=1), w_far[2], w_far[3]]
-    far_parts = [finish(w, False) for w in far_sets]
-    far_ends = [jnp.concatenate([part[flip] for part in far_parts], axis=1) for flip in range(2)]
-    same, across = [jnp.where(half == side, n, f) for n, f in zip(near_ends, far_ends)]
+            rows = slice(flip * tok, (flip + 1) * tok)
+            got = [lax.ppermute(parts[turn][rows], BOTH, moves(flip, turn)) for turn in (1, 0)]
+            ends[flip].append((got[0].astype(jnp.float32) + got[1].astype(jnp.float32)).astype(jnp.bfloat16))
+    same, across = [jnp.concatenate(pieces, axis=1) for pieces in ends]
     odd = lax.rem(seq, 2) == 1
     return jnp.concatenate([jnp.where(odd, across, same), jnp.where(odd, same, across)], axis=1)
 

time: 413 us -> 427 us (1.034)
  starting transfers between devices: 155 us -> 135 us
  waiting for transfers between devices: 154 us -> 169 us
  local copies, waits for them, and re-layouts: 17.7 us -> 27.5 us
  matrix products: 13.6 us -> 19.1 us
    ppermute x4, waiting for transfers between devices: 40.9 us -> 57.8 us  [halves_body(): lax.ppermute(part, 'seq', [(s, s ^ group) for s in range(devices)])]
    ppermute x16 -> x10, starting transfers between devices: 25.1 us -> 9.14 us  [the longest x8 9.13 us: halves_body(): lax.ppermute(parts[turn][rows], BOTH, moves(flip, turn))]
    convert_element_type x4 -> x2, local copies, waits for them, and re-layouts: 0.36 us -> 6.57 us  [halves_body(): lax.dynamic_slice_in_dim(terms, (1 - core) * 2 * tok, 2 * tok, 0)]
    dot_general x4 -> x2, matrix products: 13.6 us -> 19.1 us  [halves_body(): terms = jnp.dot(attn, weights, preferred_element_type=jnp.float32)]
    ppermute x16 -> x10, waiting for transfers between devices: 33.4 us -> 30.4 us  [the longest x8 30.4 us: halves_body(): lax.ppermute(parts[turn][rows], BOTH, moves(flip, turn))]
    unnamed x77 -> x71, local copies, waits for them, and re-layouts: 10.4 us -> 11.6 us
  transfers between devices with their start and end apart: 51 -> 45, of which waited for: 17 -> 16; matrix products, arithmetic and copies ran while one was open for 6% -> 4% of each run, Pallas kernels for 14% -> 13%
where the time goes in v1:
time: 427 us; the launch traced here: 425 us
  waiting for transfers between devices  169 us (40%)
  starting transfers between devices  135 us (32%)
  Pallas kernels  61.4 us (14%)
  local copies, waits for them, and re-layouts  27.5 us (6%)
  matrix products  19.1 us (4%)
  other arithmetic  11.3 us (3%)
    ppermute x21, starting transfers between devices, halves_body(): arrived[t][d] = lax.ppermute(piece, 'seq', [(s, s ^ d) for s in senders])  86.7 us
    ppermute x4, waiting for transfers between devices, halves_body(): lax.ppermute(part, 'seq', [(s, s ^ group) for s in range(devices)])  57.8 us
    pallas_call x3, Pallas kernels, attend_head(): pl.pallas_call(functools.partial(attention_kernel, devices, asked, tok),...  55.8 us
    ppermute x21, waiting for transfers between devices, halves_body(): arrived[t][d] = lax.ppermute(piece, 'seq', [(s, s ^ d) for s in senders])  50 us
    ppermute x8, waiting for transfers between devices, halves_body(): lax.ppermute(parts[turn][rows], BOTH, moves(flip, turn))  30.4 us
    ppermute x4, starting transfers between devices, halves_body(): lax.ppermute(part, 'seq', [(s, s ^ group) for s in range(devices)])  21.6 us
    ppermute x6, waiting for transfers between devices, halves_body(): lax.ppermute(mixed[t], 'seq', [(s, s ^ e) for s in range(devices)])  20.9 us
    dot_general x2, matrix products, halves_body(): terms = jnp.dot(attn, weights, preferred_element_type=jnp.float32)  19.1 us
  transfers between devices with their start and end apart: 45, of which 16 were waited for; matrix products, arithmetic and copies ran while one was open for 4% of the time, Pallas kernels for 13%

profile of v1, /device:TPU:0, one launch (start us, length us, event | category | flops | bytes accessed | tf_op | source)
XLA Modules:
  0.0 424.6 jit_solution(6164484218932414603)
XLA Ops:
  9.0 8.0 %collective-permute-start.10 = (bf16[1040,128]{1,0:T(8,128)(2,1)}, bf16[1040,128]{1,0:T(8,128)(2,1)S(1)}, u32[]{:S(2)}, u32[]{:S(2)}) collective-permute-start(bf16[1040,128]{1,0:T(8,128)(2,1)} %get-tuple-element.37), channel_id=1, source_target_pairs={{0,28},{4,24},{8,20},{12,16},{16,12},{20,8},{1,29},{5,25},{9,21},{... | collective-permute-start | bytes 798728 | tf_op jit(solution)/shard_map/ppermute | solution.py:215
  18.3 6.4 %collective-permute-start.8 = (bf16[1040,128]{1,0:T(8,128)(2,1)}, bf16[1040,128]{1,0:T(8,128)(2,1)S(1)}, u32[]{:S(2)}, u32[]{:S(2)}) collective-permute-start(bf16[1040,128]{1,0:T(8,128)(2,1)} %get-tuple-element.35), channel_id=1, source_target_pairs={{0,24},{4,28},{8,16},{12,20},{16,8},{20,12},{1,25},{5,29},{9,17},{... | collective-permute-start | bytes 798728 | tf_op jit(solution)/shard_map/ppermute | solution.py:215
  33.4 14.4 %collective-permute-start.1 = (bf16[1552,128]{1,0:T(8,128)(2,1)}, bf16[1552,128]{1,0:T(8,128)(2,1)S(1)}, u32[]{:S(2)}, u32[]{:S(2)}) collective-permute-start(bf16[1552,128]{1,0:T(8,128)(2,1)} %get-tuple-element.28), channel_id=1, source_target_pairs={{0,8},{4,12},{8,0},{12,4},{16,24},{20,28},{24,16},{28,20},{1,9},{5... | collective-permute-start | bytes 1191944 | tf_op jit(solution)/shard_map/ppermute | solution.py:215
  49.2 14.8 %collective-permute-start.6 = (bf16[1040,128]{1,0:T(8,128)(2,1)}, bf16[1040,128]{1,0:T(8,128)(2,1)S(1)}, u32[]{:S(2)}, u32[]{:S(2)}) collective-permute-start(bf16[1040,128]{1,0:T(8,128)(2,1)} %get-tuple-element.33), channel_id=1, source_target_pairs={{0,20},{4,16},{8,28},{12,24},{16,4},{20,0},{1,21},{5,17},{9,29},{1... | collective-permute-start | bytes 798728 | tf_op jit(solution)/shard_map/ppermute | solution.py:215
  77.9 9.1 %collective-permute-done.2.refs_3_ = bf16[1552,128]{1,0:T(8,128)(2,1)S(1)} collective-permute-done((bf16[1552,128]{1,0:T(8,128)(2,1)}, bf16[1552,128]{1,0:T(8,128)(2,1)S(1)}, u32[]{:S(2)}, u32[]{:S(2)}) %collective-permute-start.2) | collective-permute-done | bytes 397344 | tf_op jit(solution)/shard_map/ppermute | solution.py:215
  101.9 6.1 %collective-permute-done.4.refs_4_ = bf16[1040,128]{1,0:T(8,128)(2,1)S(1)} collective-permute-done((bf16[1040,128]{1,0:T(8,128)(2,1)}, bf16[1040,128]{1,0:T(8,128)(2,1)S(1)}, u32[]{:S(2)}, u32[]{:S(2)}) %collective-permute-start.4) | collective-permute-done | bytes 266272 | tf_op jit(solution)/shard_map/ppermute | solution.py:215
  113.6 8.7 %collective-permute-done.12.refs_2_ = bf16[1552,128]{1,0:T(8,128)(2,1)} collective-permute-done((bf16[1552,128]{1,0:T(8,128)(2,1)}, bf16[1552,128]{1,0:T(8,128)(2,1)}, u32[]{:S(2)}, u32[]{:S(2)}) %collective-permute-start.12) | collective-permute-done | bytes 397344 | tf_op jit(solution)/shard_map/ppermute | solution.py:215
  124.2 12.7 %collective-permute-done.13.refs_3_ = bf16[1552,128]{1,0:T(8,128)(2,1)} collective-permute-done((bf16[1552,128]{1,0:T(8,128)(2,1)}, bf16[1552,128]{1,0:T(8,128)(2,1)}, u32[]{:S(2)}, u32[]{:S(2)}) %collective-permute-start.13) | collective-permute-done | bytes 397344 | tf_op jit(solution)/shard_map/ppermute | solution.py:215
  139.9 29.9 %attend_head.3 = bf16[4096,128]{1,0:T(8,128)(2,1)S(1)} custom-call(s32[16]{0:T(128)S(1)} %broadcast_select_fusion.10.count, s32[256]{0:T(256)S(1)} %reshape.123.order, bf16[1552,128]{1,0:T(8,128)(2,1)S(1)} %copy-done.7, bf16[1552,128]{1,0:T(8,128)(2,1)S(1)} %copy-done.13, bf16[1552,128]{1,0:T(8,128)(2,1)} %collective-permute-done.12.refs_2_, ...), custom_call_target="tpu_custom_call" | custom-call | flops 8589934592 | bytes 4194304 | tf_op jit(solution)/shard_map/attend_head/pallas_call | solution.py:95
  175.9 13.5 %attend_head.4 = bf16[2048,128]{1,0:T(8,128)(2,1)S(1)} custom-call(s32[16]{0:T(128)S(1)} %get-tuple-element.47.count, s32[256]{0:T(256)S(1)} %reshape.123.order, bf16[1552,128]{1,0:T(8,128)(2,1)S(1)} %copy-done.3, bf16[1552,128]{1,0:T(8,128)(2,1)S(1)} %copy-done.5, bf16[1552,128]{1,0:T(8,128)(2,1)S(1)} %copy-done.9, bf16[1552,128]{1,0:T(8,128)(2,1)S(1)} %copy-done.11, ...), custom_call_target="tpu_custom_call" | custom-call | flops 4294967296 | bytes 3145728 | tf_op jit(solution)/shard_map/attend_head/pallas_call | solution.py:95
  190.8 8.7 %collective-permute-start.21 = (bf16[1040,128]{1,0:T(8,128)(2,1)S(1)}, bf16[1040,128]{1,0:T(8,128)(2,1)S(1)}, u32[]{:S(2)}, u32[]{:S(2)}) collective-permute-start(bf16[1040,128]{1,0:T(8,128)(2,1)S(1)} %copy-done.28), channel_id=1, source_target_pairs={{0,28},{4,24},{8,20},{12,16},{16,12},{20,8},{1,29},{5,25},{9,21},{... | collective-permute-start | bytes 798728 | tf_op jit(solution)/shard_map/ppermute | solution.py:215
  209.8 7.1 %collective-permute-start.26 = (bf16[2048,128]{1,0:T(8,128)(2,1)S(1)}, bf16[2048,128]{1,0:T(8,128)(2,1)S(1)}, u32[]{:S(2)}, u32[]{:S(2)}) collective-permute-start(bf16[2048,128]{1,0:T(8,128)(2,1)S(1)} %attend_head.4), channel_id=1, source_target_pairs={{0,8},{4,12},{8,0},{12,4},{16,24},{20,28},{24,16},{28,20},{1,9},{5... | collective-permute-start | bytes 1572872 | tf_op jit(solution)/shard_map/ppermute | solution.py:245
  217.9 12.4 %attend_head.5 = bf16[2048,128]{1,0:T(8,128)(2,1)S(1)} custom-call(s32[16]{0:T(128)S(1)} %get-tuple-element.47.count, s32[256]{0:T(256)S(1)} %reshape.123.order, bf16[1552,128]{1,0:T(8,128)(2,1)S(1)} %copy-done.2, bf16[1552,128]{1,0:T(8,128)(2,1)} %collective-permute-done.15.refs_1_, bf16[1552,128]{1,0:T(8,128)(2,1)} %collective-permute-done.16.refs_2_, ...), custom_call_target="tpu_custom_call" | custom-call | flops 4294967296 | bytes 3145728 | tf_op jit(solution)/shard_map/attend_head/pallas_call | solution.py:95
  234.1 10.5 %collective-permute-start.32 = (bf16[1536,256]{1,0:T(8,128)(2,1)S(1)}, bf16[1536,256]{1,0:T(8,128)(2,1)S(1)}, u32[]{:S(2)}, u32[]{:S(2)}) collective-permute-start(bf16[1536,256]{1,0:T(8,128)(2,1)S(1)} %copy-done.17), channel_id=1, source_target_pairs={{0,16},{4,20},{8,24},{12,28},{16,0},{20,4},{24,8},{28,12},{1,17},{... | collective-permute-start | bytes 2359304 | tf_op jit(solution)/shard_map/ppermute | solution.py:233
  244.6 8.3 %collective-permute-start.31 = (bf16[1536,128]{1,0:T(8,128)(2,1)S(1)}, bf16[1536,128]{1,0:T(8,128)(2,1)S(1)}, u32[]{:S(2)}, u32[]{:S(2)}) collective-permute-start(bf16[1536,128]{1,0:T(8,128)(2,1)S(1)} %copy-done.18), channel_id=1, source_target_pairs={{0,16},{4,20},{8,24},{12,28},{16,0},{20,4},{24,8},{28,12},{1,17},{... | collective-permute-start | bytes 1179656 | tf_op jit(solution)/shard_map/ppermute | solution.py:233
  253.9 13.3 %collective-permute-done.27 = bf16[2048,128]{1,0:T(8,128)(2,1)S(1)} collective-permute-done((bf16[2048,128]{1,0:T(8,128)(2,1)S(1)}, bf16[2048,128]{1,0:T(8,128)(2,1)S(1)}, u32[]{:S(2)}, u32[]{:S(2)}) %collective-permute-start.27) | collective-permute-done | bytes 524320 | tf_op jit(solution)/shard_map/ppermute | solution.py:245
  268.2 7.6 %collective-permute-done.25 = bf16[2048,128]{1,0:T(8,128)(2,1)S(1)} collective-permute-done((bf16[2048,128]{1,0:T(8,128)(2,1)S(1)}, bf16[2048,128]{1,0:T(8,128)(2,1)S(1)}, u32[]{:S(2)}, u32[]{:S(2)}) %collective-permute-start.25) | collective-permute-done | bytes 524320 | tf_op jit(solution)/shard_map/ppermute | solution.py:245
  277.4 10.2 %collective-permute-done.28 = bf16[2048,128]{1,0:T(8,128)(2,1)S(1)} collective-permute-done((bf16[2048,128]{1,0:T(8,128)(2,1)S(1)}, bf16[2048,128]{1,0:T(8,128)(2,1)S(1)}, u32[]{:S(2)}, u32[]{:S(2)}) %collective-permute-start.28) | collective-permute-done | bytes 524320 | tf_op jit(solution)/shard_map/ppermute | solution.py:246
  288.1 5.9 %collective-permute-done.31 = bf16[1536,128]{1,0:T(8,128)(2,1)S(1)} collective-permute-done((bf16[1536,128]{1,0:T(8,128)(2,1)S(1)}, bf16[1536,128]{1,0:T(8,128)(2,1)S(1)}, u32[]{:S(2)}, u32[]{:S(2)}) %collective-permute-start.31) | collective-permute-done | bytes 393248 | tf_op jit(solution)/shard_map/ppermute | solution.py:233
  294.0 8.0 %fusion = f32[2048,768]{1,0:T(8,128)} fusion(bf16[1536,256]{1,0:T(8,128)(2,1)S(1)} %collective-permute-done.32, bf16[1536,128]{1,0:T(8,128)(2,1)S(1)} %collective-permute-done.31, bf16[1536,384]{1,0:T(8,128)(2,1)S(1)} %copy-done.16, bf16[512,1536]{1,0:T(8,128)(2,1)S(1)} %get-tuple-element.74, bf16[512,1536]{1,0:T(8,128)(2,1)S(1)} %get-tuple-element.75, ...), kind=kOutput, calls=%fused_computation.6 | convolution fusion | flops 4864081920 | bytes 14942208 | tf_op jit(solution)/shard_map/dot_general | solution.py:274
  308.3 51.9 %collective-permute-done.37 = bf16[1536,128]{1,0:T(8,128)(2,1)} collective-permute-done((bf16[1536,128]{1,0:T(8,128)(2,1)}, bf16[1536,128]{1,0:T(8,128)(2,1)}, u32[]{:S(2)}, u32[]{:S(2)}) %collective-permute-start.37) | collective-permute-done | bytes 393248 | tf_op jit(solution)/shard_map/ppermute | solution.py:233
  365.9 11.1 %fusion.6 = f32[2048,768]{1,0:T(8,128)} fusion(bf16[1536,768]{1,0:T(8,128)(2,1)S(1)} %pad_maximum_fusion.2, bf16[512,1536]{1,0:T(8,128)(2,1)S(1)} %copy-done.22, bf16[512,1536]{1,0:T(8,128)(2,1)S(1)} %copy-done.24, bf16[512,1536]{1,0:T(8,128)(2,1)S(1)} %copy-done.26, bf16[512,1536]{1,0:T(8,128)(2,1)S(1)} %copy-done.20), kind=kOutput, calls=%fused_computation.14 | convolution fusion | flops 4857004032 | bytes 14942208 | tf_op jit(solution)/shard_map/dot_general | solution.py:274
  389.3 11.9 %collective-permute-done.34 = bf16[512,384]{1,0:T(8,128)(2,1)S(1)} collective-permute-done((bf16[512,384]{1,0:T(8,128)(2,1)S(1)}, bf16[512,384]{1,0:T(8,128)(2,1)S(1)}, u32[]{:S(2)}, u32[]{:S(2)}) %collective-permute-start.34) | collective-permute-done | bytes 393248 | tf_op jit(solution)/shard_map/ppermute | solution.py:283
  406.0 14.7 %collective-permute-done.39 = bf16[512,384]{1,0:T(8,128)(2,1)S(1)} collective-permute-done((bf16[512,384]{1,0:T(8,128)(2,1)S(1)}, bf16[512,384]{1,0:T(8,128)(2,1)S(1)}, u32[]{:S(2)}, u32[]{:S(2)}) %collective-permute-start.39) | collective-permute-done | bytes 393248 | tf_op jit(solution)/shard_map/ppermute | solution.py:283
  (195 shorter events, 118.5 us)
Async XLA Ops:
  7.7 41.5 %collective-permute-start.9 = (bf16[1552,128]{1,0:T(8,128)(2,1)}, bf16[1552,128]{1,0:T(8,128)(2,1)S(1)}, u32[]{:S(2)}, u32[]{:S(2)}) collective-permute-start(bf16[1552,128]{1,0:T(8,128)(2,1)} %get-tuple-element.36), channel_id=1, source_target_pairs={{16,12},{20,8},{24,4},{28,0},{17,13},{21,9},{25,5},{29,1},{18,14},... | collective-permute-start | bytes 1191944 | tf_op jit(solution)/shard_map/ppermute | solution.py:215
  17.0 47.0 %collective-permute-start.7 = (bf16[1552,128]{1,0:T(8,128)(2,1)}, bf16[1552,128]{1,0:T(8,128)(2,1)S(1)}, u32[]{:S(2)}, u32[]{:S(2)}) collective-permute-start(bf16[1552,128]{1,0:T(8,128)(2,1)} %get-tuple-element.34), channel_id=1, source_target_pairs={{16,8},{20,12},{24,0},{28,4},{17,9},{21,13},{25,1},{29,5},{18,10},... | collective-permute-start | bytes 1191944 | tf_op jit(solution)/shard_map/ppermute | solution.py:215
  18.3 29.6 %collective-permute-start.8 = (bf16[1040,128]{1,0:T(8,128)(2,1)}, bf16[1040,128]{1,0:T(8,128)(2,1)S(1)}, u32[]{:S(2)}, u32[]{:S(2)}) collective-permute-start(bf16[1040,128]{1,0:T(8,128)(2,1)} %get-tuple-element.35), channel_id=1, source_target_pairs={{0,24},{4,28},{8,16},{12,20},{16,8},{20,12},{1,25},{5,29},{9,17},{... | collective-permute-start | bytes 798728 | tf_op jit(solution)/shard_map/ppermute | solution.py:215
  24.7 44.8 %collective-permute-start = (bf16[1552,128]{1,0:T(8,128)(2,1)}, bf16[1552,128]{1,0:T(8,128)(2,1)S(1)}, u32[]{:S(2)}, u32[]{:S(2)}) collective-permute-start(bf16[1552,128]{1,0:T(8,128)(2,1)} %get-tuple-element.27), channel_id=1, source_target_pairs={{0,4},{4,0},{8,12},{12,8},{16,20},{20,16},{24,28},{28,24},{1,5},{5... | collective-permute-start | bytes 1191944 | tf_op jit(solution)/shard_map/ppermute | solution.py:215
  33.4 37.4 %collective-permute-start.1 = (bf16[1552,128]{1,0:T(8,128)(2,1)}, bf16[1552,128]{1,0:T(8,128)(2,1)S(1)}, u32[]{:S(2)}, u32[]{:S(2)}) collective-permute-start(bf16[1552,128]{1,0:T(8,128)(2,1)} %get-tuple-element.28), channel_id=1, source_target_pairs={{0,8},{4,12},{8,0},{12,4},{16,24},{20,28},{24,16},{28,20},{1,9},{5... | collective-permute-start | bytes 1191944 | tf_op jit(solution)/shard_map/ppermute | solution.py:215
  47.9 49.1 %collective-permute-start.5 = (bf16[1552,128]{1,0:T(8,128)(2,1)}, bf16[1552,128]{1,0:T(8,128)(2,1)S(1)}, u32[]{:S(2)}, u32[]{:S(2)}) collective-permute-start(bf16[1552,128]{1,0:T(8,128)(2,1)} %get-tuple-element.32), channel_id=1, source_target_pairs={{16,4},{20,0},{24,12},{28,8},{17,5},{21,1},{25,13},{29,9},{18,6},{... | collective-permute-start | bytes 1191944 | tf_op jit(solution)/shard_map/ppermute | solution.py:215
  49.2 45.9 %collective-permute-start.6 = (bf16[1040,128]{1,0:T(8,128)(2,1)}, bf16[1040,128]{1,0:T(8,128)(2,1)S(1)}, u32[]{:S(2)}, u32[]{:S(2)}) collective-permute-start(bf16[1040,128]{1,0:T(8,128)(2,1)} %get-tuple-element.33), channel_id=1, source_target_pairs={{0,20},{4,16},{8,28},{12,24},{16,4},{20,0},{1,21},{5,17},{9,29},{1... | collective-permute-start | bytes 798728 | tf_op jit(solution)/shard_map/ppermute | solution.py:215
  69.5 39.5 %collective-permute-start.3 = (bf16[1552,128]{1,0:T(8,128)(2,1)S(1)}, bf16[1552,128]{1,0:T(8,128)(2,1)S(1)}, u32[]{:S(2)}, u32[]{:S(2)}) collective-permute-start(bf16[1552,128]{1,0:T(8,128)(2,1)S(1)} %copy-done.6), channel_id=1, source_target_pairs={{16,0},{20,4},{24,8},{28,12},{17,1},{21,5},{25,9},{29,13},{18,2},{... | collective-permute-start | bytes 1191944 | tf_op jit(solution)/shard_map/ppermute | solution.py:215
  70.8 37.2 %collective-permute-start.4 = (bf16[1040,128]{1,0:T(8,128)(2,1)}, bf16[1040,128]{1,0:T(8,128)(2,1)S(1)}, u32[]{:S(2)}, u32[]{:S(2)}) collective-permute-start(bf16[1040,128]{1,0:T(8,128)(2,1)} %get-tuple-element.31), channel_id=1, source_target_pairs={{0,16},{4,20},{8,24},{12,28},{16,0},{20,4},{1,17},{5,21},{9,25},{1... | collective-permute-start | bytes 798728 | tf_op jit(solution)/shard_map/ppermute | solution.py:215
  97.1 39.9 %collective-permute-start.13 = (bf16[1552,128]{1,0:T(8,128)(2,1)}, bf16[1552,128]{1,0:T(8,128)(2,1)}, u32[]{:S(2)}, u32[]{:S(2)}) collective-permute-start(bf16[1552,128]{1,0:T(8,128)(2,1)} %get-tuple-element.36), channel_id=1, source_target_pairs={{0,12},{4,8},{8,4},{12,0},{1,13},{5,9},{9,5},{13,1},{2,14},{6,10},... | collective-permute-start | bytes 1191944 | tf_op jit(solution)/shard_map/ppermute | solution.py:215
  108.0 108.9 %collective-permute-start.15 = (bf16[1552,128]{1,0:T(8,128)(2,1)}, bf16[1552,128]{1,0:T(8,128)(2,1)}, u32[]{:S(2)}, u32[]{:S(2)}) collective-permute-start(bf16[1552,128]{1,0:T(8,128)(2,1)} %get-tuple-element.39), channel_id=1, source_target_pairs={{0,4},{4,0},{8,12},{12,8},{16,20},{20,16},{24,28},{28,24},{1,5},{5... | collective-permute-start | bytes 1191944 | tf_op jit(solution)/shard_map/ppermute | solution.py:215
  109.0 108.9 %collective-permute-start.16 = (bf16[1552,128]{1,0:T(8,128)(2,1)}, bf16[1552,128]{1,0:T(8,128)(2,1)}, u32[]{:S(2)}, u32[]{:S(2)}) collective-permute-start(bf16[1552,128]{1,0:T(8,128)(2,1)} %get-tuple-element.40), channel_id=1, source_target_pairs={{0,8},{4,12},{8,0},{12,4},{16,24},{20,28},{24,16},{28,20},{1,9},{5... | collective-permute-start | bytes 1191944 | tf_op jit(solution)/shard_map/ppermute | solution.py:215
  111.7 77.7 %collective-permute-start.18 = (bf16[1040,128]{1,0:T(8,128)(2,1)}, bf16[1040,128]{1,0:T(8,128)(2,1)}, u32[]{:S(2)}, u32[]{:S(2)}) collective-permute-start(bf16[1040,128]{1,0:T(8,128)(2,1)} %get-tuple-element.42), channel_id=1, source_target_pairs={{0,16},{4,20},{8,24},{12,28},{16,0},{20,4},{1,17},{5,21},{9,25},{1... | collective-permute-start | bytes 798728 | tf_op jit(solution)/shard_map/ppermute | solution.py:215
  122.3 67.2 %collective-permute-start.19 = (bf16[1040,128]{1,0:T(8,128)(2,1)}, bf16[1040,128]{1,0:T(8,128)(2,1)}, u32[]{:S(2)}, u32[]{:S(2)}) collective-permute-start(bf16[1040,128]{1,0:T(8,128)(2,1)} %get-tuple-element.43), channel_id=1, source_target_pairs={{0,20},{4,16},{8,28},{12,24},{16,4},{20,0},{1,21},{5,17},{9,29},{1... | collective-permute-start | bytes 798728 | tf_op jit(solution)/shard_map/ppermute | solution.py:215
  209.8 43.2 %collective-permute-start.26 = (bf16[2048,128]{1,0:T(8,128)(2,1)S(1)}, bf16[2048,128]{1,0:T(8,128)(2,1)S(1)}, u32[]{:S(2)}, u32[]{:S(2)}) collective-permute-start(bf16[2048,128]{1,0:T(8,128)(2,1)S(1)} %attend_head.4), channel_id=1, source_target_pairs={{0,8},{4,12},{8,0},{12,4},{16,24},{20,28},{24,16},{28,20},{1,9},{5... | collective-permute-start | bytes 1572872 | tf_op jit(solution)/shard_map/ppermute | solution.py:245
  231.4 35.8 %collective-permute-start.27 = (bf16[2048,128]{1,0:T(8,128)(2,1)S(1)}, bf16[2048,128]{1,0:T(8,128)(2,1)S(1)}, u32[]{:S(2)}, u32[]{:S(2)}) collective-permute-start(bf16[2048,128]{1,0:T(8,128)(2,1)S(1)} %attend_head.5), channel_id=1, source_target_pairs={{0,8},{4,12},{8,0},{12,4},{16,24},{20,28},{24,16},{28,20},{1,9},{5... | collective-permute-start | bytes 1572872 | tf_op jit(solution)/shard_map/ppermute | solution.py:245
  231.7 44.2 %collective-permute-start.25 = (bf16[2048,128]{1,0:T(8,128)(2,1)S(1)}, bf16[2048,128]{1,0:T(8,128)(2,1)S(1)}, u32[]{:S(2)}, u32[]{:S(2)}) collective-permute-start(bf16[2048,128]{1,0:T(8,128)(2,1)S(1)} %slice_select_fusion), channel_id=1, source_target_pairs={{0,8},{4,12},{8,0},{12,4},{16,24},{20,28},{24,16},{28,20},{1,9},{5... | collective-permute-start | bytes 1572872 | tf_op jit(solution)/shard_map/ppermute | solution.py:245
  234.1 59.9 %collective-permute-start.32 = (bf16[1536,256]{1,0:T(8,128)(2,1)S(1)}, bf16[1536,256]{1,0:T(8,128)(2,1)S(1)}, u32[]{:S(2)}, u32[]{:S(2)}) collective-permute-start(bf16[1536,256]{1,0:T(8,128)(2,1)S(1)} %copy-done.17), channel_id=1, source_target_pairs={{0,16},{4,20},{8,24},{12,28},{16,0},{20,4},{24,8},{28,12},{1,17},{... | collective-permute-start | bytes 2359304 | tf_op jit(solution)/shard_map/ppermute | solution.py:233
  244.6 49.3 %collective-permute-start.31 = (bf16[1536,128]{1,0:T(8,128)(2,1)S(1)}, bf16[1536,128]{1,0:T(8,128)(2,1)S(1)}, u32[]{:S(2)}, u32[]{:S(2)}) collective-permute-start(bf16[1536,128]{1,0:T(8,128)(2,1)S(1)} %copy-done.18), channel_id=1, source_target_pairs={{0,16},{4,20},{8,24},{12,28},{16,0},{20,4},{24,8},{28,12},{1,17},{... | collective-permute-start | bytes 1179656 | tf_op jit(solution)/shard_map/ppermute | solution.py:233
  252.9 34.8 %collective-permute-start.29 = (bf16[2048,128]{1,0:T(8,128)(2,1)S(1)}, bf16[2048,128]{1,0:T(8,128)(2,1)S(1)}, u32[]{:S(2)}, u32[]{:S(2)}) collective-permute-start(bf16[2048,128]{1,0:T(8,128)(2,1)S(1)} %collective-permute-done.26), channel_id=1, source_target_pairs={{0,4},{4,0},{8,12},{12,8},{16,20},{20,16},{24,28},{28,24},{1,5},{5... | collective-permute-start | bytes 1572872 | tf_op jit(solution)/shard_map/ppermute | solution.py:246
  305.4 56.1 %collective-permute-start.33 = (bf16[1024,768]{1,0:T(8,128)(2,1)}, bf16[1024,768]{1,0:T(8,128)(2,1)S(1)}, u32[]{:S(2)}, u32[]{:S(2)}) collective-permute-start(bf16[1024,768]{1,0:T(8,128)(2,1)} %dynamic-slice_convert_fusion.1), channel_id=1, source_target_pairs={{0,1},{1,0},{2,3},{3,2},{4,5},{5,4},{6,7},{7,6},{8,9},{9,8},{10,11... | collective-permute-start | bytes 4718600 | tf_op jit(solution)/shard_map/ppermute | solution.py:277
  305.4 54.9 %collective-permute-start.36 = (bf16[1536,256]{1,0:T(8,128)(2,1)}, bf16[1536,256]{1,0:T(8,128)(2,1)S(1)}, u32[]{:S(2)}, u32[]{:S(2)}) collective-permute-start(bf16[1536,256]{1,0:T(8,128)(2,1)} %get-tuple-element.54), channel_id=1, source_target_pairs={{0,16},{4,20},{8,24},{12,28},{16,0},{20,4},{24,8},{28,12},{1,17},{... | collective-permute-start | bytes 2359304 | tf_op jit(solution)/shard_map/ppermute | solution.py:233
  305.4 54.9 %collective-permute-start.37 = (bf16[1536,128]{1,0:T(8,128)(2,1)}, bf16[1536,128]{1,0:T(8,128)(2,1)}, u32[]{:S(2)}, u32[]{:S(2)}) collective-permute-start(bf16[1536,128]{1,0:T(8,128)(2,1)} %get-tuple-element.52), channel_id=1, source_target_pairs={{0,16},{4,20},{8,24},{12,28},{16,0},{20,4},{24,8},{28,12},{1,17},{... | collective-permute-start | bytes 1179656 | tf_op jit(solution)/shard_map/ppermute | solution.py:233
  387.2 33.5 %collective-permute-start.39 = (bf16[512,384]{1,0:T(8,128)(2,1)S(1)}, bf16[512,384]{1,0:T(8,128)(2,1)S(1)}, u32[]{:S(2)}, u32[]{:S(2)}) collective-permute-start(bf16[512,384]{1,0:T(8,128)(2,1)S(1)} %get-tuple-element.69), channel_id=1, source_target_pairs={{0,6},{1,14},{2,4},{3,12},{4,2},{5,10},{6,0},{7,8},{8,15},{9,7},{1... | collective-permute-start | bytes 1179656 | tf_op jit(solution)/shard_map/ppermute | solution.py:283
  (51 other events, 697.8 us)

commit v2 on v1

--- a/solution.py
+++ b/solution.py
@@ -268,9 +268,10 @@
     ends = [[], []]
     for p in range(2):
         first, last = bounds[2 * p], bounds[2 * p + 2]
-        weights = jnp.concatenate([w_here[:, first:last], *w_far[2 * p : 2 * p + 2]], axis=1)
+        arrived_w = w_far[2 * p : 2 * p + 2]
         if p:
-            weights = lax.optimization_barrier((weights, parts))[0]
+            arrived_w = lax.optimization_barrier((*arrived_w, *ends[0]))[:2]
+        weights = jnp.concatenate([w_here[:, first:last], *arrived_w], axis=1)
         terms = jnp.dot(attn, weights, preferred_element_type=jnp.float32)
         kept = lax.dynamic_slice_in_dim(terms, core * 2 * tok, 2 * tok, 0)
         given = lax.dynamic_slice_in_dim(terms, (1 - core) * 2 * tok, 2 * tok, 0).astype(jnp.bfloat16)

time: 427 us -> 410 us (0.960)
  local copies, waits for them, and re-layouts: 27.5 us -> 22.1 us
  matrix products: 19.1 us -> 14.4 us
    ppermute x4, waiting for transfers between devices: 57.8 us -> 42.4 us  [halves_body(): lax.ppermute(part, 'seq', [(s, s ^ group) for s in range(devices)])]
    ppermute x8, waiting for transfers between devices: 30.4 us -> 40.9 us  [halves_body(): lax.ppermute(parts[turn][rows], BOTH, moves(flip, turn))]
    dot_general x2, matrix products: 19.1 us -> 14.4 us  [halves_body(): terms = jnp.dot(attn, weights, preferred_element_type=jnp.float32)]
    convert_element_type x2, local copies, waits for them, and re-layouts: 6.57 us -> 2.21 us  [halves_body(): lax.dynamic_slice_in_dim(terms, (1 - core) * 2 * tok, 2 * tok, 0)]
    unnamed x71 -> x73, local copies, waits for them, and re-layouts: 11.6 us -> 9.82 us
  transfers between devices with their start and end apart: 45 -> 45, of which waited for: 16 -> 19; matrix products, arithmetic and copies ran while one was open for 4% -> 4% of each run, Pallas kernels for 13% -> 14%
where the time goes in v2:
time: 410 us; the launch traced here: 409 us
  waiting for transfers between devices  169 us (41%)
  starting transfers between devices  132 us (32%)
  Pallas kernels  61.4 us (15%)
  local copies, waits for them, and re-layouts  22.1 us (5%)
  matrix products  14.4 us (4%)
  other arithmetic  9.37 us (2%)
    ppermute x21, starting transfers between devices, halves_body(): arrived[t][d] = lax.ppermute(piece, 'seq', [(s, s ^ d) for s in senders])  86.6 us
    pallas_call x3, Pallas kernels, attend_head(): pl.pallas_call(functools.partial(attention_kernel, devices, asked, tok),...  55.7 us
    ppermute x21, waiting for transfers between devices, halves_body(): arrived[t][d] = lax.ppermute(piece, 'seq', [(s, s ^ d) for s in senders])  50 us
    ppermute x4, waiting for transfers between devices, halves_body(): lax.ppermute(part, 'seq', [(s, s ^ group) for s in range(devices)])  42.4 us
    ppermute x8, waiting for transfers between devices, halves_body(): lax.ppermute(parts[turn][rows], BOTH, moves(flip, turn))  40.9 us
    ppermute x6, waiting for transfers between devices, halves_body(): lax.ppermute(mixed[t], 'seq', [(s, s ^ e) for s in range(devices)])  21.1 us
    ppermute x4, starting transfers between devices, halves_body(): lax.ppermute(part, 'seq', [(s, s ^ group) for s in range(devices)])  18.9 us
    dot_general x2, matrix products, halves_body(): terms = jnp.dot(attn, weights, preferred_element_type=jnp.float32)  14.4 us
  transfers between devices with their start and end apart: 45, of which 19 were waited for; matrix products, arithmetic and copies ran while one was open for 4% of the time, Pallas kernels for 14%

profile of v2, /device:TPU:0, one launch (start us, length us, event | category | flops | bytes accessed | tf_op | source)
XLA Modules:
  0.0 408.8 jit_solution(14888288984172934578)
XLA Ops:
  9.1 7.9 %collective-permute-start.10 = (bf16[1040,128]{1,0:T(8,128)(2,1)}, bf16[1040,128]{1,0:T(8,128)(2,1)S(1)}, u32[]{:S(2)}, u32[]{:S(2)}) collective-permute-start(bf16[1040,128]{1,0:T(8,128)(2,1)} %get-tuple-element.38), channel_id=1, source_target_pairs={{0,28},{4,24},{8,20},{12,16},{16,12},{20,8},{1,29},{5,25},{9,21},{... | collective-permute-start | bytes 798728 | tf_op jit(solution)/shard_map/ppermute | solution.py:215
  18.4 6.4 %collective-permute-start.8 = (bf16[1040,128]{1,0:T(8,128)(2,1)}, bf16[1040,128]{1,0:T(8,128)(2,1)S(1)}, u32[]{:S(2)}, u32[]{:S(2)}) collective-permute-start(bf16[1040,128]{1,0:T(8,128)(2,1)} %get-tuple-element.36), channel_id=1, source_target_pairs={{0,24},{4,28},{8,16},{12,20},{16,8},{20,12},{1,25},{5,29},{9,17},{... | collective-permute-start | bytes 798728 | tf_op jit(solution)/shard_map/ppermute | solution.py:215
  33.5 14.4 %collective-permute-start.1 = (bf16[1552,128]{1,0:T(8,128)(2,1)}, bf16[1552,128]{1,0:T(8,128)(2,1)S(1)}, u32[]{:S(2)}, u32[]{:S(2)}) collective-permute-start(bf16[1552,128]{1,0:T(8,128)(2,1)} %get-tuple-element.29), channel_id=1, source_target_pairs={{0,8},{4,12},{8,0},{12,4},{16,24},{20,28},{24,16},{28,20},{1,9},{5... | collective-permute-start | bytes 1191944 | tf_op jit(solution)/shard_map/ppermute | solution.py:215
  49.3 14.8 %collective-permute-start.6 = (bf16[1040,128]{1,0:T(8,128)(2,1)}, bf16[1040,128]{1,0:T(8,128)(2,1)S(1)}, u32[]{:S(2)}, u32[]{:S(2)}) collective-permute-start(bf16[1040,128]{1,0:T(8,128)(2,1)} %get-tuple-element.34), channel_id=1, source_target_pairs={{0,20},{4,16},{8,28},{12,24},{16,4},{20,0},{1,21},{5,17},{9,29},{1... | collective-permute-start | bytes 798728 | tf_op jit(solution)/shard_map/ppermute | solution.py:215
  77.8 9.2 %collective-permute-done.2.refs_3_ = bf16[1552,128]{1,0:T(8,128)(2,1)S(1)} collective-permute-done((bf16[1552,128]{1,0:T(8,128)(2,1)}, bf16[1552,128]{1,0:T(8,128)(2,1)S(1)}, u32[]{:S(2)}, u32[]{:S(2)}) %collective-permute-start.2) | collective-permute-done | bytes 397344 | tf_op jit(solution)/shard_map/ppermute | solution.py:215
  101.9 6.1 %collective-permute-done.4.refs_4_ = bf16[1040,128]{1,0:T(8,128)(2,1)S(1)} collective-permute-done((bf16[1040,128]{1,0:T(8,128)(2,1)}, bf16[1040,128]{1,0:T(8,128)(2,1)S(1)}, u32[]{:S(2)}, u32[]{:S(2)}) %collective-permute-start.4) | collective-permute-done | bytes 266272 | tf_op jit(solution)/shard_map/ppermute | solution.py:215
  113.6 8.7 %collective-permute-done.12.refs_2_ = bf16[1552,128]{1,0:T(8,128)(2,1)} collective-permute-done((bf16[1552,128]{1,0:T(8,128)(2,1)}, bf16[1552,128]{1,0:T(8,128)(2,1)}, u32[]{:S(2)}, u32[]{:S(2)}) %collective-permute-start.12) | collective-permute-done | bytes 397344 | tf_op jit(solution)/shard_map/ppermute | solution.py:215
  124.3 12.7 %collective-permute-done.13.refs_3_ = bf16[1552,128]{1,0:T(8,128)(2,1)} collective-permute-done((bf16[1552,128]{1,0:T(8,128)(2,1)}, bf16[1552,128]{1,0:T(8,128)(2,1)}, u32[]{:S(2)}, u32[]{:S(2)}) %collective-permute-start.13) | collective-permute-done | bytes 397344 | tf_op jit(solution)/shard_map/ppermute | solution.py:215
  139.9 29.9 %attend_head.3 = bf16[4096,128]{1,0:T(8,128)(2,1)S(1)} custom-call(s32[16]{0:T(128)S(1)} %broadcast_select_fusion.10.count, s32[256]{0:T(256)S(1)} %reshape.123.order, bf16[1552,128]{1,0:T(8,128)(2,1)S(1)} %copy-done.7, bf16[1552,128]{1,0:T(8,128)(2,1)S(1)} %copy-done.13, bf16[1552,128]{1,0:T(8,128)(2,1)} %collective-permute-done.12.refs_2_, ...), custom_call_target="tpu_custom_call" | custom-call | flops 8589934592 | bytes 4194304 | tf_op jit(solution)/shard_map/attend_head/pallas_call | solution.py:95
  175.8 13.5 %attend_head.4 = bf16[2048,128]{1,0:T(8,128)(2,1)S(1)} custom-call(s32[16]{0:T(128)S(1)} %get-tuple-element.49.count, s32[256]{0:T(256)S(1)} %reshape.123.order, bf16[1552,128]{1,0:T(8,128)(2,1)S(1)} %copy-done.3, bf16[1552,128]{1,0:T(8,128)(2,1)S(1)} %copy-done.5, bf16[1552,128]{1,0:T(8,128)(2,1)S(1)} %copy-done.9, bf16[1552,128]{1,0:T(8,128)(2,1)S(1)} %copy-done.11, ...), custom_call_target="tpu_custom_call" | custom-call | flops 4294967296 | bytes 3145728 | tf_op jit(solution)/shard_map/attend_head/pallas_call | solution.py:95
  190.8 8.7 %collective-permute-start.21 = (bf16[1040,128]{1,0:T(8,128)(2,1)S(1)}, bf16[1040,128]{1,0:T(8,128)(2,1)S(1)}, u32[]{:S(2)}, u32[]{:S(2)}) collective-permute-start(bf16[1040,128]{1,0:T(8,128)(2,1)S(1)} %copy-done.29), channel_id=1, source_target_pairs={{0,28},{4,24},{8,20},{12,16},{16,12},{20,8},{1,29},{5,25},{9,21},{... | collective-permute-start | bytes 798728 | tf_op jit(solution)/shard_map/ppermute | solution.py:215
  209.7 7.2 %collective-permute-start.26 = (bf16[2048,128]{1,0:T(8,128)(2,1)S(1)}, bf16[2048,128]{1,0:T(8,128)(2,1)S(1)}, u32[]{:S(2)}, u32[]{:S(2)}) collective-permute-start(bf16[2048,128]{1,0:T(8,128)(2,1)S(1)} %attend_head.4), channel_id=1, source_target_pairs={{0,8},{4,12},{8,0},{12,4},{16,24},{20,28},{24,16},{28,20},{1,9},{5... | collective-permute-start | bytes 1572872 | tf_op jit(solution)/shard_map/ppermute | solution.py:245
  217.9 12.4 %attend_head.5 = bf16[2048,128]{1,0:T(8,128)(2,1)S(1)} custom-call(s32[16]{0:T(128)S(1)} %get-tuple-element.49.count, s32[256]{0:T(256)S(1)} %reshape.123.order, bf16[1552,128]{1,0:T(8,128)(2,1)S(1)} %copy-done.2, bf16[1552,128]{1,0:T(8,128)(2,1)} %collective-permute-done.15.refs_1_, bf16[1552,128]{1,0:T(8,128)(2,1)} %collective-permute-done.16.refs_2_, ...), custom_call_target="tpu_custom_call" | custom-call | flops 4294967296 | bytes 3145728 | tf_op jit(solution)/shard_map/attend_head/pallas_call | solution.py:95
  234.1 10.4 %collective-permute-start.32 = (bf16[1536,256]{1,0:T(8,128)(2,1)S(1)}, bf16[1536,256]{1,0:T(8,128)(2,1)S(1)}, u32[]{:S(2)}, u32[]{:S(2)}) collective-permute-start(bf16[1536,256]{1,0:T(8,128)(2,1)S(1)} %copy-done.17), channel_id=1, source_target_pairs={{0,16},{4,20},{8,24},{12,28},{16,0},{20,4},{24,8},{28,12},{1,17},{... | collective-permute-start | bytes 2359304 | tf_op jit(solution)/shard_map/ppermute | solution.py:233
  244.6 8.3 %collective-permute-start.31 = (bf16[1536,128]{1,0:T(8,128)(2,1)S(1)}, bf16[1536,128]{1,0:T(8,128)(2,1)S(1)}, u32[]{:S(2)}, u32[]{:S(2)}) collective-permute-start(bf16[1536,128]{1,0:T(8,128)(2,1)S(1)} %copy-done.19), channel_id=1, source_target_pairs={{0,16},{4,20},{8,24},{12,28},{16,0},{20,4},{24,8},{28,12},{1,17},{... | collective-permute-start | bytes 1179656 | tf_op jit(solution)/shard_map/ppermute | solution.py:233
  253.9 13.3 %collective-permute-done.27 = bf16[2048,128]{1,0:T(8,128)(2,1)S(1)} collective-permute-done((bf16[2048,128]{1,0:T(8,128)(2,1)S(1)}, bf16[2048,128]{1,0:T(8,128)(2,1)S(1)}, u32[]{:S(2)}, u32[]{:S(2)}) %collective-permute-start.27) | collective-permute-done | bytes 524320 | tf_op jit(solution)/shard_map/ppermute | solution.py:245
  268.2 7.7 %collective-permute-done.25 = bf16[2048,128]{1,0:T(8,128)(2,1)S(1)} collective-permute-done((bf16[2048,128]{1,0:T(8,128)(2,1)S(1)}, bf16[2048,128]{1,0:T(8,128)(2,1)S(1)}, u32[]{:S(2)}, u32[]{:S(2)}) %collective-permute-start.25) | collective-permute-done | bytes 524320 | tf_op jit(solution)/shard_map/ppermute | solution.py:245
  277.4 10.3 %collective-permute-done.28 = bf16[2048,128]{1,0:T(8,128)(2,1)S(1)} collective-permute-done((bf16[2048,128]{1,0:T(8,128)(2,1)S(1)}, bf16[2048,128]{1,0:T(8,128)(2,1)S(1)}, u32[]{:S(2)}, u32[]{:S(2)}) %collective-permute-start.28) | collective-permute-done | bytes 524320 | tf_op jit(solution)/shard_map/ppermute | solution.py:246
  288.1 5.8 %collective-permute-done.31 = bf16[1536,128]{1,0:T(8,128)(2,1)S(1)} collective-permute-done((bf16[1536,128]{1,0:T(8,128)(2,1)S(1)}, bf16[1536,128]{1,0:T(8,128)(2,1)S(1)}, u32[]{:S(2)}, u32[]{:S(2)}) %collective-permute-start.31) | collective-permute-done | bytes 393248 | tf_op jit(solution)/shard_map/ppermute | solution.py:233
  293.9 8.1 %fusion = f32[2048,768]{1,0:T(8,128)} fusion(bf16[1536,256]{1,0:T(8,128)(2,1)S(1)} %collective-permute-done.32, bf16[1536,128]{1,0:T(8,128)(2,1)S(1)} %collective-permute-done.31, bf16[1536,384]{1,0:T(8,128)(2,1)S(1)} %copy-done.16, bf16[512,1536]{1,0:T(8,128)(2,1)S(1)} %get-tuple-element.76, bf16[512,1536]{1,0:T(8,128)(2,1)S(1)} %get-tuple-element.77, ...), kind=kOutput, calls=%fused_computation.6 | convolution fusion | flops 4864081920 | bytes 14942208 | tf_op jit(solution)/shard_map/dot_general | solution.py:275
  312.4 9.9 %collective-permute-done.38 = bf16[512,384]{1,0:T(8,128)(2,1)S(1)} collective-permute-done((bf16[512,384]{1,0:T(8,128)(2,1)S(1)}, bf16[512,384]{1,0:T(8,128)(2,1)S(1)}, u32[]{:S(2)}, u32[]{:S(2)}) %collective-permute-start.38) | collective-permute-done | bytes 393248 | tf_op jit(solution)/shard_map/ppermute | solution.py:284
  322.3 36.6 %collective-permute-done.37 = bf16[1536,128]{1,0:T(8,128)(2,1)S(1)} collective-permute-done((bf16[1536,128]{1,0:T(8,128)(2,1)S(1)}, bf16[1536,128]{1,0:T(8,128)(2,1)S(1)}, u32[]{:S(2)}, u32[]{:S(2)}) %collective-permute-start.37) | collective-permute-done | bytes 393248 | tf_op jit(solution)/shard_map/ppermute | solution.py:233
  358.9 6.4 %fusion.6 = f32[2048,768]{1,0:T(8,128)S(1)} fusion(bf16[1536,128]{1,0:T(8,128)(2,1)S(1)} %collective-permute-done.37, bf16[1536,256]{1,0:T(8,128)(2,1)} %collective-permute-done.36, bf16[1536,384]{1,0:T(8,128)(2,1)S(1)} %copy-done.15, bf16[512,1536]{1,0:T(8,128)(2,1)S(1)} %copy-done.23, bf16[512,1536]{1,0:T(8,128)(2,1)S(1)} %copy-done.25, ...), kind=kOutput, calls=%fused_computation.12 | convolution fusion | flops 4864081920 | bytes 14942208 | tf_op jit(solution)/shard_map/dot_general | solution.py:275
  374.1 20.8 %collective-permute-done.34 = bf16[512,384]{1,0:T(8,128)(2,1)S(1)} collective-permute-done((bf16[512,384]{1,0:T(8,128)(2,1)S(1)}, bf16[512,384]{1,0:T(8,128)(2,1)S(1)}, u32[]{:S(2)}, u32[]{:S(2)}) %collective-permute-start.34) | collective-permute-done | bytes 393248 | tf_op jit(solution)/shard_map/ppermute | solution.py:284
  (196 shorter events, 118.6 us)
Async XLA Ops:
  7.8 41.4 %collective-permute-start.9 = (bf16[1552,128]{1,0:T(8,128)(2,1)}, bf16[1552,128]{1,0:T(8,128)(2,1)S(1)}, u32[]{:S(2)}, u32[]{:S(2)}) collective-permute-start(bf16[1552,128]{1,0:T(8,128)(2,1)} %get-tuple-element.37), channel_id=1, source_target_pairs={{16,12},{20,8},{24,4},{28,0},{17,13},{21,9},{25,5},{29,1},{18,14},... | collective-permute-start | bytes 1191944 | tf_op jit(solution)/shard_map/ppermute | solution.py:215
  17.1 47.0 %collective-permute-start.7 = (bf16[1552,128]{1,0:T(8,128)(2,1)}, bf16[1552,128]{1,0:T(8,128)(2,1)S(1)}, u32[]{:S(2)}, u32[]{:S(2)}) collective-permute-start(bf16[1552,128]{1,0:T(8,128)(2,1)} %get-tuple-element.35), channel_id=1, source_target_pairs={{16,8},{20,12},{24,0},{28,4},{17,9},{21,13},{25,1},{29,5},{18,10},... | collective-permute-start | bytes 1191944 | tf_op jit(solution)/shard_map/ppermute | solution.py:215
  24.7 44.7 %collective-permute-start = (bf16[1552,128]{1,0:T(8,128)(2,1)}, bf16[1552,128]{1,0:T(8,128)(2,1)S(1)}, u32[]{:S(2)}, u32[]{:S(2)}) collective-permute-start(bf16[1552,128]{1,0:T(8,128)(2,1)} %get-tuple-element.28), channel_id=1, source_target_pairs={{0,4},{4,0},{8,12},{12,8},{16,20},{20,16},{24,28},{28,24},{1,5},{5... | collective-permute-start | bytes 1191944 | tf_op jit(solution)/shard_map/ppermute | solution.py:215
  33.5 37.3 %collective-permute-start.1 = (bf16[1552,128]{1,0:T(8,128)(2,1)}, bf16[1552,128]{1,0:T(8,128)(2,1)S(1)}, u32[]{:S(2)}, u32[]{:S(2)}) collective-permute-start(bf16[1552,128]{1,0:T(8,128)(2,1)} %get-tuple-element.29), channel_id=1, source_target_pairs={{0,8},{4,12},{8,0},{12,4},{16,24},{20,28},{24,16},{28,20},{1,9},{5... | collective-permute-start | bytes 1191944 | tf_op jit(solution)/shard_map/ppermute | solution.py:215
  48.0 49.1 %collective-permute-start.5 = (bf16[1552,128]{1,0:T(8,128)(2,1)}, bf16[1552,128]{1,0:T(8,128)(2,1)S(1)}, u32[]{:S(2)}, u32[]{:S(2)}) collective-permute-start(bf16[1552,128]{1,0:T(8,128)(2,1)} %get-tuple-element.33), channel_id=1, source_target_pairs={{16,4},{20,0},{24,12},{28,8},{17,5},{21,1},{25,13},{29,9},{18,6},{... | collective-permute-start | bytes 1191944 | tf_op jit(solution)/shard_map/ppermute | solution.py:215
  49.3 45.9 %collective-permute-start.6 = (bf16[1040,128]{1,0:T(8,128)(2,1)}, bf16[1040,128]{1,0:T(8,128)(2,1)S(1)}, u32[]{:S(2)}, u32[]{:S(2)}) collective-permute-start(bf16[1040,128]{1,0:T(8,128)(2,1)} %get-tuple-element.34), channel_id=1, source_target_pairs={{0,20},{4,16},{8,28},{12,24},{16,4},{20,0},{1,21},{5,17},{9,29},{1... | collective-permute-start | bytes 798728 | tf_op jit(solution)/shard_map/ppermute | solution.py:215
  69.5 39.5 %collective-permute-start.3 = (bf16[1552,128]{1,0:T(8,128)(2,1)S(1)}, bf16[1552,128]{1,0:T(8,128)(2,1)S(1)}, u32[]{:S(2)}, u32[]{:S(2)}) collective-permute-start(bf16[1552,128]{1,0:T(8,128)(2,1)S(1)} %copy-done.6), channel_id=1, source_target_pairs={{16,0},{20,4},{24,8},{28,12},{17,1},{21,5},{25,9},{29,13},{18,2},{... | collective-permute-start | bytes 1191944 | tf_op jit(solution)/shard_map/ppermute | solution.py:215
  70.8 37.2 %collective-permute-start.4 = (bf16[1040,128]{1,0:T(8,128)(2,1)}, bf16[1040,128]{1,0:T(8,128)(2,1)S(1)}, u32[]{:S(2)}, u32[]{:S(2)}) collective-permute-start(bf16[1040,128]{1,0:T(8,128)(2,1)} %get-tuple-element.32), channel_id=1, source_target_pairs={{0,16},{4,20},{8,24},{12,28},{16,0},{20,4},{1,17},{5,21},{9,25},{1... | collective-permute-start | bytes 798728 | tf_op jit(solution)/shard_map/ppermute | solution.py:215
  97.1 39.9 %collective-permute-start.13 = (bf16[1552,128]{1,0:T(8,128)(2,1)}, bf16[1552,128]{1,0:T(8,128)(2,1)}, u32[]{:S(2)}, u32[]{:S(2)}) collective-permute-start(bf16[1552,128]{1,0:T(8,128)(2,1)} %get-tuple-element.37), channel_id=1, source_target_pairs={{0,12},{4,8},{8,4},{12,0},{1,13},{5,9},{9,5},{13,1},{2,14},{6,10},... | collective-permute-start | bytes 1191944 | tf_op jit(solution)/shard_map/ppermute | solution.py:215
  108.0 108.9 %collective-permute-start.15 = (bf16[1552,128]{1,0:T(8,128)(2,1)}, bf16[1552,128]{1,0:T(8,128)(2,1)}, u32[]{:S(2)}, u32[]{:S(2)}) collective-permute-start(bf16[1552,128]{1,0:T(8,128)(2,1)} %get-tuple-element.40), channel_id=1, source_target_pairs={{0,4},{4,0},{8,12},{12,8},{16,20},{20,16},{24,28},{28,24},{1,5},{5... | collective-permute-start | bytes 1191944 | tf_op jit(solution)/shard_map/ppermute | solution.py:215
  109.0 108.9 %collective-permute-start.16 = (bf16[1552,128]{1,0:T(8,128)(2,1)}, bf16[1552,128]{1,0:T(8,128)(2,1)}, u32[]{:S(2)}, u32[]{:S(2)}) collective-permute-start(bf16[1552,128]{1,0:T(8,128)(2,1)} %get-tuple-element.41), channel_id=1, source_target_pairs={{0,8},{4,12},{8,0},{12,4},{16,24},{20,28},{24,16},{28,20},{1,9},{5... | collective-permute-start | bytes 1191944 | tf_op jit(solution)/shard_map/ppermute | solution.py:215
  111.7 77.7 %collective-permute-start.18 = (bf16[1040,128]{1,0:T(8,128)(2,1)}, bf16[1040,128]{1,0:T(8,128)(2,1)}, u32[]{:S(2)}, u32[]{:S(2)}) collective-permute-start(bf16[1040,128]{1,0:T(8,128)(2,1)} %get-tuple-element.43), channel_id=1, source_target_pairs={{0,16},{4,20},{8,24},{12,28},{16,0},{20,4},{1,17},{5,21},{9,25},{1... | collective-permute-start | bytes 798728 | tf_op jit(solution)/shard_map/ppermute | solution.py:215
  122.3 67.1 %collective-permute-start.19 = (bf16[1040,128]{1,0:T(8,128)(2,1)}, bf16[1040,128]{1,0:T(8,128)(2,1)}, u32[]{:S(2)}, u32[]{:S(2)}) collective-permute-start(bf16[1040,128]{1,0:T(8,128)(2,1)} %get-tuple-element.44), channel_id=1, source_target_pairs={{0,20},{4,16},{8,28},{12,24},{16,4},{20,0},{1,21},{5,17},{9,29},{1... | collective-permute-start | bytes 798728 | tf_op jit(solution)/shard_map/ppermute | solution.py:215
  209.7 43.2 %collective-permute-start.26 = (bf16[2048,128]{1,0:T(8,128)(2,1)S(1)}, bf16[2048,128]{1,0:T(8,128)(2,1)S(1)}, u32[]{:S(2)}, u32[]{:S(2)}) collective-permute-start(bf16[2048,128]{1,0:T(8,128)(2,1)S(1)} %attend_head.4), channel_id=1, source_target_pairs={{0,8},{4,12},{8,0},{12,4},{16,24},{20,28},{24,16},{28,20},{1,9},{5... | collective-permute-start | bytes 1572872 | tf_op jit(solution)/shard_map/ppermute | solution.py:245
  231.4 35.8 %collective-permute-start.27 = (bf16[2048,128]{1,0:T(8,128)(2,1)S(1)}, bf16[2048,128]{1,0:T(8,128)(2,1)S(1)}, u32[]{:S(2)}, u32[]{:S(2)}) collective-permute-start(bf16[2048,128]{1,0:T(8,128)(2,1)S(1)} %attend_head.5), channel_id=1, source_target_pairs={{0,8},{4,12},{8,0},{12,4},{16,24},{20,28},{24,16},{28,20},{1,9},{5... | collective-permute-start | bytes 1572872 | tf_op jit(solution)/shard_map/ppermute | solution.py:245
  231.7 44.2 %collective-permute-start.25 = (bf16[2048,128]{1,0:T(8,128)(2,1)S(1)}, bf16[2048,128]{1,0:T(8,128)(2,1)S(1)}, u32[]{:S(2)}, u32[]{:S(2)}) collective-permute-start(bf16[2048,128]{1,0:T(8,128)(2,1)S(1)} %slice_select_fusion), channel_id=1, source_target_pairs={{0,8},{4,12},{8,0},{12,4},{16,24},{20,28},{24,16},{28,20},{1,9},{5... | collective-permute-start | bytes 1572872 | tf_op jit(solution)/shard_map/ppermute | solution.py:245
  234.1 59.9 %collective-permute-start.32 = (bf16[1536,256]{1,0:T(8,128)(2,1)S(1)}, bf16[1536,256]{1,0:T(8,128)(2,1)S(1)}, u32[]{:S(2)}, u32[]{:S(2)}) collective-permute-start(bf16[1536,256]{1,0:T(8,128)(2,1)S(1)} %copy-done.17), channel_id=1, source_target_pairs={{0,16},{4,20},{8,24},{12,28},{16,0},{20,4},{24,8},{28,12},{1,17},{... | collective-permute-start | bytes 2359304 | tf_op jit(solution)/shard_map/ppermute | solution.py:233
  244.6 49.3 %collective-permute-start.31 = (bf16[1536,128]{1,0:T(8,128)(2,1)S(1)}, bf16[1536,128]{1,0:T(8,128)(2,1)S(1)}, u32[]{:S(2)}, u32[]{:S(2)}) collective-permute-start(bf16[1536,128]{1,0:T(8,128)(2,1)S(1)} %copy-done.19), channel_id=1, source_target_pairs={{0,16},{4,20},{8,24},{12,28},{16,0},{20,4},{24,8},{28,12},{1,17},{... | collective-permute-start | bytes 1179656 | tf_op jit(solution)/shard_map/ppermute | solution.py:233
  252.9 34.9 %collective-permute-start.29 = (bf16[2048,128]{1,0:T(8,128)(2,1)S(1)}, bf16[2048,128]{1,0:T(8,128)(2,1)S(1)}, u32[]{:S(2)}, u32[]{:S(2)}) collective-permute-start(bf16[2048,128]{1,0:T(8,128)(2,1)S(1)} %collective-permute-done.26), channel_id=1, source_target_pairs={{0,4},{4,0},{8,12},{12,8},{16,20},{20,16},{24,28},{28,24},{1,5},{5... | collective-permute-start | bytes 1572872 | tf_op jit(solution)/shard_map/ppermute | solution.py:246
  304.1 54.8 %collective-permute-start.36 = (bf16[1536,256]{1,0:T(8,128)(2,1)}, bf16[1536,256]{1,0:T(8,128)(2,1)}, u32[]{:S(2)}, u32[]{:S(2)}) collective-permute-start(bf16[1536,256]{1,0:T(8,128)(2,1)} %get-tuple-element.56), channel_id=1, source_target_pairs={{0,16},{4,20},{8,24},{12,28},{16,0},{20,4},{24,8},{28,12},{1,17},{... | collective-permute-start | bytes 2359304 | tf_op jit(solution)/shard_map/ppermute | solution.py:233
  312.3 46.6 %collective-permute-start.37 = (bf16[1536,128]{1,0:T(8,128)(2,1)S(1)}, bf16[1536,128]{1,0:T(8,128)(2,1)S(1)}, u32[]{:S(2)}, u32[]{:S(2)}) collective-permute-start(bf16[1536,128]{1,0:T(8,128)(2,1)S(1)} %copy-done.18), channel_id=1, source_target_pairs={{0,16},{4,20},{8,24},{12,28},{16,0},{20,4},{24,8},{28,12},{1,17},{... | collective-permute-start | bytes 1179656 | tf_op jit(solution)/shard_map/ppermute | solution.py:233
  369.7 32.6 %collective-permute-start.41 = (bf16[512,384]{1,0:T(8,128)(2,1)S(1)}, bf16[512,384]{1,0:T(8,128)(2,1)S(1)}, u32[]{:S(2)}, u32[]{:S(2)}) collective-permute-start(bf16[512,384]{1,0:T(8,128)(2,1)S(1)} %get-tuple-element.71), channel_id=1, source_target_pairs={{0,6},{1,14},{2,4},{3,12},{4,2},{5,10},{6,0},{7,8},{8,15},{9,7},{1... | collective-permute-start | bytes 1179656 | tf_op jit(solution)/shard_map/ppermute | solution.py:284
  372.6 33.3 %collective-permute-start.42 = (bf16[512,384]{1,0:T(8,128)(2,1)}, bf16[512,384]{1,0:T(8,128)(2,1)}, u32[]{:S(2)}, u32[]{:S(2)}) collective-permute-start(bf16[512,384]{1,0:T(8,128)(2,1)} %get-tuple-element.73), channel_id=1, source_target_pairs={{0,4},{1,12},{2,6},{3,14},{4,0},{5,8},{6,2},{7,10},{8,13},{9,5},{1... | collective-permute-start | bytes 1179656 | tf_op jit(solution)/shard_map/ppermute | solution.py:284
  373.0 34.1 %collective-permute-start.43 = (bf16[512,384]{1,0:T(8,128)(2,1)S(1)}, bf16[512,384]{1,0:T(8,128)(2,1)S(1)}, u32[]{:S(2)}, u32[]{:S(2)}) collective-permute-start(bf16[512,384]{1,0:T(8,128)(2,1)S(1)} %get-tuple-element.72), channel_id=1, source_target_pairs={{0,2},{1,10},{2,0},{3,8},{4,6},{5,14},{6,4},{7,12},{8,11},{9,3},{1... | collective-permute-start | bytes 1179656 | tf_op jit(solution)/shard_map/ppermute | solution.py:284
  (52 other events, 861.4 us)
